TPU v7x, 128 devices: a whole 4x4x4 slice. The times are simulated.
128 devices in a mesh: rep: 16 (over x, z), ctx: 8 (over y, core).
Axes of the slice: x: 4, y: 4, z: 4, core: 2. Of those that a mesh axis runs over, the one named last changes fastest.
Arguments:
- pre_query: bfloat16 [16, 4096, 2048], P('rep', 'ctx'), may hold values from -6 to 6
- pre_pairs: bfloat16 [16, 2, 4096, 1024], P('rep', None, 'ctx'), may hold values from -6 to 6
- prefill_len: int32 [16], P('rep'), may hold values from 2048 to 4096
- dec_query: bfloat16 [256, 2048], P('rep'), may hold values from -6 to 6
- dec_own: bfloat16 [256, 2, 1024], P('rep'), may hold values from -6 to 6
- cache: bfloat16 [256, 2, 1024, 1024], P('rep', None, 'ctx'), may hold values from -6 to 6
- cached_len: int32 [256], replicated, may hold values from 1 to 1024, as said below
- move: int32 [256], replicated, may hold values from 0 to 255, as said below
Outputs:
- pre_out: bfloat16 [16, 4096, 2048], P('rep', 'ctx')
- dec_out: bfloat16 [256, 2048], P('rep')
Inputs may be any that keep to these rules, and one draw needn't show every extreme that they name: `cached_len`: some request has exactly 1024 cached positions. move is a permutation of 0 to 255; slot s lies on replica s // 16, request r has home replica r // 16, and move[r] % 16 == r % 16. The 16 requests of one replica go one to each replica, and the 16 slots of one replica serve one request of each replica.
All inputs are finite; a program needn't handle non-finite values.
Results may differ from a plain program's by a relative error of at most 0.0095.
Values may be sent and summed in bfloat16 or wider, within the bound.
No kernel may reach another device: no remote copies, remote signals or barrier semaphores. Data moves between devices by JAX's collectives and lax.ppermute only.
A program may use at most 128 MiB of HBM per device.

v0:
```python
import functools
import math

import jax
import jax.numpy as jnp
from jax import lax
from jax.experimental import pallas as pl
from jax.experimental.pallas import tpu as pltpu
from jax.sharding import PartitionSpec as P


QH = 16
KVH = 8
HD = 128
SCALE = 1.0 / 12.0
EXP2_SCALE = SCALE * math.log2(math.e)
MASKED = -1e30
TILE = 128
CHUNK = 1024
VMEM = 63_000_000
SMALL = 20_000_000
BF16 = jnp.bfloat16
F32 = jnp.float32


def swap(array, flip):
    return lax.ppermute(array, "ctx", [(i, i ^ flip) for i in range(8)])


def exchange(array):
    return lax.all_to_all(array, "rep", split_axis=0, concat_axis=0, tiled=True)


def lanes(array, at, width):
    return lax.dynamic_slice_in_dim(array, at * width, width, axis=array.ndim - 1)


def attend_kernel(table, *refs, key_pieces, value_pieces, query_pieces, blocks, out_sizes, count_in):
    inputs = refs[:count_in]
    out_refs = refs[count_in : count_in + len(out_sizes)]
    token = refs[count_in + len(out_sizes)]
    keys, values, queries, mixes, acc, top, sems, out_sems = refs[count_in + len(out_sizes) + 1 :]
    me = table[0]
    valid = table[1]
    core = me & 1
    copies = []

    def view(piece):
        which, index, kind = piece
        ref = inputs[which]
        if index is not None:
            ref = ref.at[index]
        if kind == "own":
            ref = ref.at[:, pl.ds(pl.multiple_of(me * HD, HD), HD)]
        elif kind == "core":
            ref = ref.at[:, pl.ds(pl.multiple_of(core * HD, HD), HD)]
        elif kind == "query":
            ref = ref.at[:, pl.ds(pl.multiple_of(me * 2 * HD, 2 * HD), 2 * HD)]
        return ref

    def put(piece, dest):
        copy = pltpu.make_async_copy(view(piece), dest, sems.at[len(copies)])
        copy.start()
        copies.append(copy)

    for z, piece in enumerate(key_pieces):
        at = pl.multiple_of((me ^ z) * 512, 512)
        put(piece, keys.at[pl.ds(at, 512)])
    for z, piece in enumerate(value_pieces):
        at = pl.multiple_of((me ^ z) * 512, 512)
        put(piece, values.at[pl.ds(at, 512), 0:HD])
    for n, piece in enumerate(query_pieces):
        put(piece, queries.at[n])
    values[:, HD:] = jnp.ones((values.shape[0], HD), BF16)
    for copy in copies:
        copy.wait()

    halves = 1
    parts = [(t, slice(t * TILE, (t + 1) * TILE)) for t in range(512 // TILE)]

    def one_block(n, block):
        first = block * 512

        @pl.when(first >= valid)
        def _():
            mixes[n] = jnp.zeros((512, 2 * HD), BF16)

        @pl.when(first < valid)
        def _():
            rest = first % CHUNK
            base = pl.multiple_of(first - rest, CHUNK)

            for start in range(0, CHUNK, 512):

                @pl.when(rest == start)
                def _(start=start):
                    for t, rows in parts:
                        width = start + (t + 1) * TILE
                        key = keys[pl.ds(base, width)]
                        value = values[pl.ds(base, width)]
                        seen = lax.broadcasted_iota(
                            jnp.int32, (TILE, width), 1
                        ) <= lax.broadcasted_iota(jnp.int32, (TILE, width), 0) + (width - TILE)
                        for g in range(2):
                            query = queries[n, rows, g * HD : (g + 1) * HD]
                            score = lax.dot_general(
                                query, key, (((1,), (1,)), ((), ())), preferred_element_type=F32
                            )
                            score = jnp.where(seen, score, MASKED)
                            new_top = jnp.max(score, axis=1, keepdims=True)
                            top[g, rows] = jnp.broadcast_to(new_top, (TILE, HD))
                            weight = jnp.exp2((score - new_top) * EXP2_SCALE).astype(BF16)
                            acc[g, rows] = jnp.dot(weight, value, preferred_element_type=F32)

            def full(step, unused):
                at = pl.multiple_of((step // halves) * CHUNK, CHUNK)
                half = (step % halves) * (512 // halves)
                key = keys[pl.ds(at, CHUNK)]
                value = values[pl.ds(at, CHUNK)]
                for t in range(512 // TILE // halves):
                    rows = pl.ds(pl.multiple_of(half + t * TILE, TILE), TILE)
                    for g in range(2):
                        query = queries[n, rows, g * HD : (g + 1) * HD]
                        score = lax.dot_general(
                            query, key, (((1,), (1,)), ((), ())), preferred_element_type=F32
                        )
                        old_top = top[g, rows]
                        new_top = jnp.maximum(old_top, jnp.max(score, axis=1, keepdims=True))
                        factor = jnp.exp2((old_top - new_top) * EXP2_SCALE)
                        top[g, rows] = new_top
                        weight = jnp.exp2((score - new_top[:, :1]) * EXP2_SCALE).astype(BF16)
                        more = jnp.dot(weight, value, preferred_element_type=F32)
                        acc[g, rows, :HD] = acc[g, rows, :HD] * factor + more[:, :HD]
                        acc[g, rows, HD:] = acc[g, rows, HD:] * factor + more[:, HD:]
                return unused

            lax.fori_loop(0, (first // CHUNK) * halves, full, 0)
            live = lax.broadcasted_iota(jnp.int32, (512, HD), 0) + first < valid
            for g in range(2):
                mixed = acc[g, :, :HD] / acc[g, :, HD:]
                mixes[n, :, g * HD : (g + 1) * HD] = jnp.where(live, mixed, 0.0).astype(BF16)

    leaving = []
    for out_ref, size in zip(out_refs, out_sizes):
        for i in range(size):
            n = len(leaving)
            leaving.append(
                pltpu.make_async_copy(mixes.at[n], out_ref.at[i], out_sems.at[n])
            )

    def step(n, unused):
        flip = jnp.int32(blocks[0])
        for more in range(1, len(blocks)):
            flip = jnp.where(n == more, blocks[more], flip)
        one_block(n, me ^ flip)
        return unused

    lax.fori_loop(0, len(blocks), step, 0)
    for copy in leaving:
        copy.start()
    for copy in leaving:
        copy.wait()
    token[...] = jnp.zeros_like(token)


def attend_call(table, arrays, key_pieces, value_pieces, query_pieces, blocks, out_sizes):
    n = len(query_pieces)
    kernel = functools.partial(
        attend_kernel,
        key_pieces=key_pieces,
        value_pieces=value_pieces,
        query_pieces=query_pieces,
        blocks=blocks,
        out_sizes=out_sizes,
        count_in=len(arrays),
    )
    return pl.pallas_call(
        kernel,
        grid_spec=pltpu.PrefetchScalarGridSpec(
            num_scalar_prefetch=1,
            grid=(1,),
            in_specs=[pl.BlockSpec(memory_space=pl.ANY)] * len(arrays),
            out_specs=[pl.BlockSpec(memory_space=pl.ANY)] * len(out_sizes)
            + [pl.BlockSpec((8, HD), lambda i, t: (0, 0))],
            scratch_shapes=[
                pltpu.VMEM((4096, HD), BF16),
                pltpu.VMEM((4096, 2 * HD), BF16),
                pltpu.VMEM((n, 512, 2 * HD), BF16),
                pltpu.VMEM((n, 512, 2 * HD), BF16),
                pltpu.VMEM((2, 512, 2 * HD), F32),
                pltpu.VMEM((2, 512, HD), F32),
                pltpu.SemaphoreType.DMA((16 + n,)),
                pltpu.SemaphoreType.DMA((n,)),
            ],
        ),
        out_shape=[jax.ShapeDtypeStruct((size, 512, 2 * HD), BF16) for size in out_sizes]
        + [jax.ShapeDtypeStruct((8, HD), F32)],
        compiler_params=pltpu.CompilerParams(vmem_limit_bytes=SMALL),
        cost_estimate=pl.CostEstimate(
            flops=n * 1_200_000_000, bytes_accessed=4_000_000, transcendentals=n * 2_000_000
        ),
    )(table, *arrays)


def collect_kernel(table, *refs, outs, count_in):
    inputs = refs[:count_in]
    out_refs = refs[count_in:-1]
    sems = refs[-1]
    me = table[0]
    copies = []
    for out_ref, pieces in zip(out_refs, outs):
        for n, (which, index, lane, out_lane, width) in enumerate(pieces):
            ref = inputs[which]
            if index is not None:
                ref = ref.at[index]
            if lane is not None:
                ref = ref.at[:, pl.ds(pl.multiple_of(lane(me) * width, width), width)]
            if out_lane is None:
                dest = out_ref.at[n]
            else:
                at = pl.multiple_of(out_lane(me) * width, width)
                dest = out_ref.at[0, :, pl.ds(at, width)]
            copy = pltpu.make_async_copy(ref, dest, sems.at[len(copies)])
            copy.start()
            copies.append(copy)
    for copy in copies:
        copy.wait()


def collect(table, arrays, outs):
    shapes = []
    for pieces in outs:
        if pieces[0][3] is None:
            shapes.append((len(pieces), 512, pieces[0][4]))
        else:
            shapes.append((1, 512, len(pieces) * pieces[0][4]))
    total = sum(math.prod(shape) for shape in shapes)
    result = pl.pallas_call(
        functools.partial(collect_kernel, outs=outs, count_in=len(arrays)),
        grid_spec=pltpu.PrefetchScalarGridSpec(
            num_scalar_prefetch=1,
            grid=(1,),
            in_specs=[pl.BlockSpec(memory_space=pl.ANY)] * len(arrays),
            out_specs=[pl.BlockSpec(shape, lambda i, t: (0, 0, 0)) for shape in shapes],
            scratch_shapes=[pltpu.SemaphoreType.DMA((sum(len(p) for p in outs),))],
        ),
        out_shape=[jax.ShapeDtypeStruct(shape, BF16) for shape in shapes],
        compiler_params=pltpu.CompilerParams(vmem_limit_bytes=SMALL),
        cost_estimate=pl.CostEstimate(
            flops=total * 2, bytes_accessed=total * 4, transcendentals=0
        ),
    )(table, *arrays)
    return result


def after(value, *others):
    return lax.optimization_barrier((value, *others))[0]


def wide(array, at):
    return lanes(array, at, 2 * HD)


def prefill_pairs(me, pre_pairs):
    chip = me >> 1
    key, value = pre_pairs[0, 0], pre_pairs[0, 1]
    key_1 = jnp.stack([wide(key, chip ^ 1), wide(key, chip ^ 2)])
    value_1 = jnp.stack([wide(value, chip ^ 3), wide(value, chip ^ 2)])
    return key_1, value_1


def prefill_pairs_on(me, pre_pairs, key_1, value_1):
    chip = me >> 1
    key, value = pre_pairs[0, 0], pre_pairs[0, 1]
    key_2 = jnp.stack([wide(key, chip ^ 3), key_1[1]])
    value_2 = jnp.stack([wide(value, chip ^ 1), value_1[1]])
    return key_2, value_2


def prefill_queries(me, query):
    query_x = swap(jnp.stack([wide(query, me ^ 7), wide(query, me ^ 5)]), 1)
    query_y = swap(jnp.stack([wide(query, me ^ 1), wide(query, me ^ 3)]), 1)
    query_a1 = jnp.stack([wide(query, me ^ 2), wide(query, me ^ 4)])
    return query_x, query_y, query_a1


def prefill_across(table, pairs, key_1, key_2, value_1, value_2):
    def other(which, index):
        return (which, index, lambda m: 1 - (m & 1), None, HD)

    def own(index):
        return (0, index, lambda m: m ^ 1, None, HD)

    (pairs_x,) = collect(
        table,
        [pairs, key_1, key_2, value_1, value_2],
        [
            [
                own(0),
                other(1, 0),
                other(2, 1),
                other(2, 0),
                own(1),
                other(4, 0),
                other(4, 1),
                other(3, 0),
            ]
        ],
    )
    return swap(pairs_x, 1)


KEY_PIECES = [
    (0, 0, "own"),
    (5, 0, None),
    (1, 0, "core"),
    (5, 1, None),
    (2, 1, "core"),
    (5, 2, None),
    (2, 0, "core"),
    (5, 3, None),
]
VALUE_PIECES = [
    (0, 1, "own"),
    (5, 4, None),
    (4, 0, "core"),
    (5, 5, None),
    (4, 1, "core"),
    (5, 6, None),
    (3, 0, "core"),
    (5, 7, None),
]


def part(table, keyed, arrays, pieces, blocks, out_sizes):
    return attend_call(table, keyed + arrays, KEY_PIECES, VALUE_PIECES, pieces, blocks, out_sizes)


def prefill_join(table, outs):
    def place(which, index, z):
        return (which, index, None, lambda m: m ^ z, 2 * HD)

    places = [(0, 0), (4, 0), (1, 1), (4, 1), (3, 0), (4, 3), (2, 0), (4, 2)]
    (joined,) = collect(
        table, outs, [[place(which, index, z) for z, (which, index) in enumerate(places)]]
    )
    return joined


def cache_kernel(table, query_ref, cache_ref, out_ref):
    span_base = table[0]
    count = query_ref.shape[0]
    step_count, span = cache_ref.shape[0], cache_ref.shape[2]
    head = lax.broadcasted_iota(jnp.int32, (QH, KVH * HD), 0) // 2
    block = lax.broadcasted_iota(jnp.int32, (QH, KVH * HD), 1) // HD
    lane = lax.broadcasted_iota(jnp.int32, (QH, HD), 1)
    position = lax.broadcasted_iota(jnp.int32, (QH, span), 1) + span_base
    rows, scores, seen = [], [], []
    for i in range(step_count):
        n = pl.program_id(0) * step_count + i
        rows.append(table[1 + count + n])
        query = query_ref[rows[i]]
        wide = jnp.where(head == block, jnp.concatenate([query] * KVH, axis=1), 0).astype(BF16)
        scores.append(
            lax.dot_general(
                wide, cache_ref[i, 0], (((1,), (1,)), ((), ())), preferred_element_type=F32
            )
        )
        seen.append(position < table[1 + n])
    visible = jnp.concatenate(seen, axis=0)
    score = jnp.where(visible, jnp.concatenate(scores, axis=0) * SCALE, MASKED)
    top = jnp.max(score, axis=1, keepdims=True).astype(BF16).astype(F32)
    weight = jnp.where(visible, jnp.exp(score - top), 0.0)
    total = jnp.sum(weight, axis=1, keepdims=True)
    weight = weight.astype(BF16)
    for i in range(step_count):
        part = slice(i * QH, (i + 1) * QH)
        mixed = jnp.dot(weight[part], cache_ref[i, 1], preferred_element_type=F32)
        mixed = jnp.where(head == block, mixed, 0.0)
        picked = mixed[:, :HD]
        for h in range(1, KVH):
            picked = picked + mixed[:, h * HD : (h + 1) * HD]
        out_ref[rows[i], :, :HD] = picked.astype(BF16)
        out_ref[rows[i], :, HD:] = jnp.where(
            lane == 0,
            jnp.broadcast_to(top[part], (QH, HD)),
            jnp.broadcast_to(total[part], (QH, HD)),
        ).astype(BF16)


def over_cache(span_base, lengths, dest_rep, queries, cache):
    count = cache.shape[0]
    span = cache.shape[2]
    each = math.gcd(count, 4)
    table = jnp.concatenate([jnp.stack([span_base]), lengths, dest_rep]).astype(jnp.int32)
    return pl.pallas_call(
        cache_kernel,
        grid_spec=pltpu.PrefetchScalarGridSpec(
            num_scalar_prefetch=1,
            grid=(count // each,),
            in_specs=[
                pl.BlockSpec((count, QH, HD), lambda n, t: (0, 0, 0)),
                pl.BlockSpec((each, 2, span, KVH * HD), lambda n, t: (n, 0, 0, 0)),
            ],
            out_specs=pl.BlockSpec((count, QH, 2 * HD), lambda n, t: (0, 0, 0)),
        ),
        out_shape=jax.ShapeDtypeStruct((count, QH, 2 * HD), BF16),
        compiler_params=pltpu.CompilerParams(vmem_limit_bytes=VMEM),
        cost_estimate=pl.CostEstimate(
            flops=8_000_000_000, bytes_accessed=8_500_000, transcendentals=300_000
        ),
        name="over_cache",
    )(table, queries, cache)


def merge(left, right):
    left, right = left.astype(F32), right.astype(F32)
    left_top, right_top = left[..., HD : HD + 1], right[..., HD : HD + 1]
    new_top = jnp.maximum(left_top, right_top)
    left_factor = jnp.exp(left_top - new_top)
    right_factor = jnp.exp(right_top - new_top)
    weighted = left[..., :HD] * left_factor + right[..., :HD] * right_factor
    total = left[..., HD + 1 : HD + 2] * left_factor + right[..., HD + 1 : HD + 2] * right_factor
    return weighted, new_top, total


def packed(weighted, top, total):
    return jnp.concatenate([weighted, top, total], axis=-1).astype(BF16)


def decode_tables(cache, cached_len, move):
    per_rep = cache.shape[0]
    rep = lax.axis_index("rep")
    requests = move.shape[0]
    ids = jnp.arange(per_rep, dtype=jnp.int32)
    dest_rep = lax.dynamic_slice_in_dim(move, rep * per_rep, per_rep) // per_rep
    lengths = lax.dynamic_slice_in_dim(cached_len, rep * per_rep, per_rep)
    my_slots = rep * per_rep + ids
    served = jnp.sum(
        jnp.where(
            move[None, :] == my_slots[:, None], jnp.arange(requests, dtype=jnp.int32)[None, :], 0
        ),
        axis=1,
    )
    return dest_rep, lengths, served // per_rep


def decode_send(source_rep, dec_query):
    reps = lax.axis_size("rep")
    to_home = jnp.arange(reps, dtype=jnp.int32)[:, None] == source_rep[None, :]
    return jnp.dot(to_home.astype(BF16), dec_query, preferred_element_type=F32).astype(BF16)


def decode_home(me, lengths, dest_rep, arrived, cache):
    reps = lax.axis_size("rep")
    span = cache.shape[2]
    partial = over_cache(me * span, lengths, dest_rep, arrived.reshape(reps, QH, HD), cache)
    return partial[:, :, : HD + 2].reshape(reps, QH * (HD + 2))


def decode_order(source_rep, back):
    reps = back.shape[0]
    back = jnp.dot(
        (source_rep[:, None] == jnp.arange(reps, dtype=jnp.int32)[None, :]).astype(BF16),
        back,
        preferred_element_type=F32,
    ).astype(BF16)
    return back.reshape(source_rep.shape[0], QH, HD + 2)


def decode_finish(weighted, top, total, dec_query, dec_own):
    per_rep = dec_query.shape[0]
    query_heads = dec_query.reshape(per_rep, KVH, 2, HD)
    own_key = dec_own[:, 0].reshape(per_rep, KVH, HD)
    own_value = dec_own[:, 1].reshape(per_rep, KVH, HD).astype(F32)
    own_score = (
        jnp.sum(query_heads.astype(F32) * own_key[:, :, None, :].astype(F32), axis=-1) * SCALE
    ).reshape(per_rep, QH, 1)
    own_value = jnp.broadcast_to(own_value[:, :, None, :], (per_rep, KVH, 2, HD)).reshape(
        per_rep, QH, HD
    )
    new_top = jnp.maximum(top, own_score)
    keep = jnp.exp(top - new_top)
    own_weight = jnp.exp(own_score - new_top)
    mixed = (weighted * keep + own_weight * own_value) / (total * keep + own_weight)
    return mixed.reshape(per_rep, QH * HD).astype(BF16)


def layer(pre_query, pre_pairs, prefill_len, dec_query, dec_own, cache, cached_len, move):
    me = lax.axis_index("ctx").astype(jnp.int32)
    table = jnp.stack([me, prefill_len[0]]).astype(jnp.int32)
    pairs, query = pre_pairs[0], pre_query[0]
    key_1, value_1 = prefill_pairs(me, pre_pairs)
    dest_rep, lengths, source_rep = decode_tables(cache, cached_len, move)
    outgoing = after(decode_send(source_rep, dec_query), key_1, value_1)
    key_1, value_1 = swap(key_1, 2), swap(value_1, 6)
    arrived = exchange(outgoing)
    key_2, value_2 = prefill_pairs_on(me, pre_pairs, key_1, value_1)
    query_later = after(query, outgoing, key_2, value_2)
    key_2, value_2 = swap(key_2, 6), swap(value_2, 2)
    query_b1, query_x, query_a1 = prefill_queries(me, query_later)
    arrived = after(arrived, query_a1)
    query_a1, query_b1 = swap(query_a1, 2), swap(query_b1, 6)
    partial = decode_home(me, lengths, dest_rep, arrived, cache)
    back = exchange(partial)
    pairs_x = prefill_across(table, pairs, key_1, key_2, value_1, value_2)
    keyed = [pairs, key_1, key_2, value_1, value_2, pairs_x]
    query_a2 = swap(jnp.stack([wide(query, me ^ 6), query_a1[1]]), 6)
    query_b2 = swap(jnp.stack([query_x[1], query_b1[1]]), 2)
    back = decode_order(source_rep, back)
    other = swap(back, 1)
    out_5, out_4, out_32, token = part(
        table,
        keyed,
        [query_a1, query_a2, query_b2, back],
        [(8, 1, None), (7, 1, None), (8, 0, None), (6, 0, None)],
        [5, 4, 3, 2],
        [1, 1, 2],
    )
    back_5, back_4 = swap(out_5, 2), swap(out_4, 6)
    back_32 = swap(out_32, 2)
    back = packed(*merge(back, other))
    other = swap(back, 2)
    out_0, out_7, token = part(
        table,
        keyed,
        [query, query_b1, back, token],
        [(6, None, "query"), (7, 0, None)],
        [0, 7],
        [1, 1],
    )
    back_5 = swap(back_5, 6)
    back_4 = swap(back_4, 2)
    back_7 = swap(out_7, 6)
    back = packed(*merge(back, other))
    other = swap(back, 6)
    out_1, out_6, token = part(
        table, keyed, [query_a2, query_x, back, token], [(7, 0, None), (6, 0, None)], [1, 6], [1, 1]
    )
    back_6 = swap(out_6, 6)
    back_x = swap(jnp.concatenate([out_1, back_32[0:1], back_7, back_5]), 1)
    pre_out = prefill_join(table, [out_0, back_32, back_6, back_4, back_x])
    weighted, top, total = merge(back, other)
    dec_out = decode_finish(weighted, top, total, dec_query, dec_own)
    return (pre_out, dec_out)


def solution(mesh):
    in_specs = (
        P("rep", "ctx", None),
        P("rep", None, "ctx", None),
        P("rep"),
        P("rep", None),
        P("rep", None, None),
        P("rep", None, "ctx", None),
        P(),
        P(),
    )
    out_specs = (P("rep", "ctx", None), P("rep", None))
    return jax.shard_map(layer, mesh=mesh, in_specs=in_specs, out_specs=out_specs, check_vma=False)
```

profile of v0, /device:TPU:2, one launch (start us, length us, event | category | flops | bytes accessed | tf_op | source)
XLA Modules:
  0.0 166.6 jit_solution(8107006623145797664)
XLA Ops:
  0.6 1.7 %fusion.33 = (bf16[1,1,512,1024]{3,2,1,0:T(8,128)(2,1)S(1)}, bf16[1,1,512,1024]{3,2,1,0:T(8,128)(2,1)S(1)}) fusion(bf16[1,2,512,1024]{3,2,1,0:T(8,128)(2,1)} %param.9), kind=kLoop, calls=%fused_computation.103 | loop fusion | bytes 4194304 | tf_op jit(solution)/shard_map/slice | solution.py:266
  4.2 1.6 collective-permute-start
  6.6 2.2 %collective-permute-start.2 = (bf16[2,512,256]{2,1,0:T(8,128)(2,1)}, bf16[2,512,256]{2,1,0:T(8,128)(2,1)S(1)}, u32[]{:S(2)}, u32[]{:S(2)}) collective-permute-start(bf16[2,512,256]{2,1,0:T(8,128)(2,1)} %pad_maximum_fusion.3), channel_id=1, source_target_pairs={{0,6},{1,7},{2,4},{3,5},{4,2},{5,3},{6,0},{7,1},{8,14},{9,15},{10,... | collective-permute-start | bytes 1572872 | tf_op jit(solution)/shard_map/ppermute | solution.py:27
  10.9 8.3 %all-to-all-start = ((bf16[16,2,1024]{2,1,0:T(2,128)(2,1)}), bf16[16,2,1024]{2,1,0:T(2,128)(2,1)}, u32[]{:S(2)}, u32[]{:S(2)}) async-start(bf16[16,2,1024]{2,1,0:T(2,128)(2,1)} %reshape.121), calls=%async_computation | async-start | bytes 131072 | tf_op jit(solution)/shard_map/all_to_all | solution.py:31
  21.4 4.2 %all-to-all-done = bf16[16,2,1024]{2,1,0:T(2,128)(2,1)} async-done(((bf16[16,2,1024]{2,1,0:T(2,128)(2,1)}), bf16[16,2,1024]{2,1,0:T(2,128)(2,1)}, u32[]{:S(2)}, u32[]{:S(2)}) %all-to-all-start) | async-done | bytes 65568 | tf_op jit(solution)/shard_map/all_to_all | solution.py:31
  26.6 1.8 %pad_maximum_fusion.2 = bf16[2,512,256]{2,1,0:T(8,128)(2,1)} fusion(bf16[1,512,256]{2,1,0:T(8,128)(2,1)S(1)} %slice.118, bf16[1,512,256]{2,1,0:T(8,128)(2,1)} %get-tuple-element.65), kind=kLoop, calls=%fused_computation.4 | loop fusion | flops 262144 | bytes 1048576 | tf_op jit(solution)/shard_map/stack | solution.py:275
  32.3 2.0 %collective-permute-start.8 = (bf16[2,512,256]{2,1,0:T(8,128)(2,1)}, bf16[2,512,256]{2,1,0:T(8,128)(2,1)}, u32[]{:S(2)}, u32[]{:S(2)}) collective-permute-start(bf16[2,512,256]{2,1,0:T(8,128)(2,1)} %pad_maximum_fusion.6), channel_id=1, source_target_pairs={{0,2},{1,3},{2,0},{3,1},{4,6},{5,7},{6,4},{7,5},{8,10},{9,11},{10,... | collective-permute-start | bytes 1572872 | tf_op jit(solution)/shard_map/ppermute | solution.py:27
  34.9 6.6 %over_cache.1 = bf16[16,16,256]{2,1,0:T(8,128)(2,1)} custom-call(s32[33]{0:T(128)} %pad_add_fusion.1.table, bf16[16,16,128]{2,1,0:T(8,128)(2,1)} %bitcast.61, bf16[16,2,128,1024]{3,2,1,0:T(8,128)(2,1)} %cache_ref.1), custom_call_target="tpu_custom_call" | custom-call | flops 8000000000 | bytes 8500000 | tf_op jit(solution)/shard_map/over_cache/pallas_call | solution.py:396
  41.5 1.2 all_to_all.22
  44.4 4.8 %all-to-all-start.1 = ((bf16[16,2,1040]{2,1,0:T(2,128)(2,1)}), bf16[16,2,1040]{2,1,0:T(2,128)(2,1)S(1)}, u32[]{:S(2)}, u32[]{:S(2)}) async-start(bf16[16,2,1040]{2,1,0:T(2,128)(2,1)} %reshape.123), calls=%async_computation.1 | async-start | bytes 147456 | tf_op jit(solution)/shard_map/all_to_all | solution.py:31
  49.3 2.0 %pad_maximum_fusion.5 = bf16[2,512,256]{2,1,0:T(8,128)(2,1)} fusion(bf16[1,512,256]{2,1,0:T(8,128)(2,1)} %get-tuple-element.45, bf16[1,512,256]{2,1,0:T(8,128)(2,1)} %get-tuple-element.46), kind=kLoop, calls=%fused_computation.7 | loop fusion | flops 262144 | bytes 1048576 | tf_op jit(solution)/shard_map/stack | solution.py:281
  51.3 4.3 %all-to-all-done.1 = bf16[16,2,1040]{2,1,0:T(2,128)(2,1)S(1)} async-done(((bf16[16,2,1040]{2,1,0:T(2,128)(2,1)}), bf16[16,2,1040]{2,1,0:T(2,128)(2,1)S(1)}, u32[]{:S(2)}, u32[]{:S(2)}) %all-to-all-start.1) | async-done | bytes 66592 | tf_op jit(solution)/shard_map/all_to_all | solution.py:31
  56.3 1.8 %convolution_convert_fusion = bf16[16,2080]{1,0:T(8,128)(2,1)} fusion(bf16[16,1,2080]{2,1,0:T(2,128)(2,1)} %reshape.124, s32[16]{0:T(128)S(1)} %get-tuple-element.62), kind=kOutput, calls=%fused_computation | convolution fusion | flops 1098496 | bytes 133184 | tf_op jit(solution)/shard_map/dot_general | solution.py:463
  58.1 1.3 reshape.107.refs_9_
  61.3 2.3 %collective-permute-start.6 = (bf16[2,512,256]{2,1,0:T(8,128)(2,1)}, bf16[2,512,256]{2,1,0:T(8,128)(2,1)S(1)}, u32[]{:S(2)}, u32[]{:S(2)}) collective-permute-start(bf16[2,512,256]{2,1,0:T(8,128)(2,1)} %collective-permute-done.5), channel_id=1, source_target_pairs={{0,6},{1,7},{2,4},{3,5},{4,2},{5,3},{6,0},{7,1},{8,14},{9,15},{10,... | collective-permute-start | bytes 1572872 | tf_op jit(solution)/shard_map/ppermute | solution.py:27
  63.7 1.8 %shard_map.95 = bf16[8,512,128]{2,1,0:T(8,128)(2,1)S(1)} custom-call(s32[2]{0:T(128)S(1)} %pad_add_fusion.table, bf16[2,512,1024]{2,1,0:T(8,128)(2,1)S(1)} %bitcast.47, bf16[2,512,256]{2,1,0:T(8,128)(2,1)S(1)} %collective-permute-done.refs_1_, bf16[2,512,256]{2,1,0:T(8,128)(2,1)} %collective-permute-done.1.refs_2_, ...), custom_call_target="tpu_custom_call" | custom-call | flops 1048576 | bytes 2097152 | tf_op jit(solution)/shard_map/pallas_call | solution.py:238
  67.0 1.1 collective-permute-start.9
  68.1 9.4 %collective-permute-done.6.refs_7_ = bf16[2,512,256]{2,1,0:T(8,128)(2,1)S(1)} collective-permute-done((bf16[2,512,256]{2,1,0:T(8,128)(2,1)}, bf16[2,512,256]{2,1,0:T(8,128)(2,1)S(1)}, u32[]{:S(2)}, u32[]{:S(2)}) %collective-permute-start.6) | collective-permute-done | bytes 524320 | tf_op jit(solution)/shard_map/ppermute | solution.py:27
  78.3 9.8 %collective-permute-done.9.refs_7_.refs_6_ = bf16[2,512,256]{2,1,0:T(8,128)(2,1)S(1)} collective-permute-done((bf16[2,512,256]{2,1,0:T(8,128)(2,1)S(1)}, bf16[2,512,256]{2,1,0:T(8,128)(2,1)S(1)}, u32[]{:S(2)}, u32[]{:S(2)}) %collective-permute-start.9) | collective-permute-done | bytes 524320 | tf_op jit(solution)/shard_map/ppermute | solution.py:27
  88.1 2.3 %collective-permute-done.11.refs_8_ = bf16[2,512,256]{2,1,0:T(8,128)(2,1)S(1)} collective-permute-done((bf16[2,512,256]{2,1,0:T(8,128)(2,1)S(1)}, bf16[2,512,256]{2,1,0:T(8,128)(2,1)S(1)}, u32[]{:S(2)}, u32[]{:S(2)}) %collective-permute-start.11) | collective-permute-done | bytes 524320 | tf_op jit(solution)/shard_map/ppermute | solution.py:27
  90.4 19.5 %shard_map.96 = (bf16[1,512,256]{2,1,0:T(8,128)(2,1)S(1)}, bf16[1,512,256]{2,1,0:T(8,128)(2,1)S(1)}, bf16[2,512,256]{2,1,0:T(8,128)(2,1)S(1)}, f32[8,128]{1,0:T(8,128)S(1)}) custom-call(s32[2]{0:T(128)S(1)} %pad_add_fusion.table, bf16[2,512,1024]{2,1,0:T(8,128)(2,1)S(1)} %bitcast.48, bf16[2,512,256]{2,1,0:T(8,128)(2,1)S(1)} %collective-permute-done.refs_1_, ...), custom_call_target="tpu_custom_call" | custom-call | flops 4800000000 | bytes 4000000 | tf_op jit(solution)/shard_map/pallas_call | solution.py:177
  110.4 1.8 %collective-permute-start.12 = (bf16[2,512,256]{2,1,0:T(8,128)(2,1)S(1)}, bf16[2,512,256]{2,1,0:T(8,128)(2,1)S(1)}, u32[]{:S(2)}, u32[]{:S(2)}) collective-permute-start(bf16[2,512,256]{2,1,0:T(8,128)(2,1)S(1)} %get-tuple-element.19), channel_id=1, source_target_pairs={{0,2},{1,3},{2,0},{3,1},{4,6},{5,7},{6,4},{7,5},{8,10},{9,11},{10,... | collective-permute-start | bytes 1572872 | tf_op jit(solution)/shard_map/ppermute | solution.py:27
  113.3 10.9 %shard_map.97 = (bf16[1,512,256]{2,1,0:T(8,128)(2,1)S(1)}, bf16[1,512,256]{2,1,0:T(8,128)(2,1)S(1)}, f32[8,128]{1,0:T(8,128)S(1)}) custom-call(s32[2]{0:T(128)S(1)} %pad_add_fusion.table, bf16[2,512,1024]{2,1,0:T(8,128)(2,1)S(1)} %bitcast.49, bf16[2,512,256]{2,1,0:T(8,128)(2,1)S(1)} %collective-permute-done.refs_1_, ...), custom_call_target="tpu_custom_call" | custom-call | flops 2400000000 | bytes 4000000 | tf_op jit(solution)/shard_map/pallas_call | solution.py:177
  124.2 2.2 %collective-permute-start.17 = (bf16[1,512,256]{2,1,0:T(8,128)(2,1)S(1)}, bf16[1,512,256]{2,1,0:T(8,128)(2,1)S(1)}, u32[]{:S(2)}, u32[]{:S(2)}) collective-permute-start(bf16[1,512,256]{2,1,0:T(8,128)(2,1)S(1)} %get-tuple-element.24), channel_id=1, source_target_pairs={{0,6},{1,7},{2,4},{3,5},{4,2},{5,3},{6,0},{7,1},{8,14},{9,15},{10,... | collective-permute-start | bytes 786440 | tf_op jit(solution)/shard_map/ppermute | solution.py:27
  128.3 11.5 %shard_map.98 = (bf16[1,512,256]{2,1,0:T(8,128)(2,1)S(1)}, bf16[1,512,256]{2,1,0:T(8,128)(2,1)S(1)}, f32[8,128]{1,0:T(8,128)}) custom-call(s32[2]{0:T(128)S(1)} %pad_add_fusion.table, bf16[2,512,1024]{2,1,0:T(8,128)(2,1)S(1)} %bitcast.50, bf16[2,512,256]{2,1,0:T(8,128)(2,1)S(1)} %collective-permute-done.refs_1_, ...), custom_call_target="tpu_custom_call" | custom-call | flops 2400000000 | bytes 4000000 | tf_op jit(solution)/shard_map/pallas_call | solution.py:177
  140.0 1.1 pad_maximum_fusion
  141.3 2.2 %collective-permute-start.15 = (bf16[1,512,256]{2,1,0:T(8,128)(2,1)S(1)}, bf16[1,512,256]{2,1,0:T(8,128)(2,1)}, u32[]{:S(2)}, u32[]{:S(2)}) collective-permute-start(bf16[1,512,256]{2,1,0:T(8,128)(2,1)S(1)} %copy-done.6), channel_id=1, source_target_pairs={{0,6},{1,7},{2,4},{3,5},{4,2},{5,3},{6,0},{7,1},{8,14},{9,15},{10,... | collective-permute-start | bytes 786440 | tf_op jit(solution)/shard_map/ppermute | solution.py:27
  143.9 1.1 collective-permute-start.21
  145.2 8.9 %collective-permute-done.21 = bf16[16,16,130]{2,1,0:T(8,128)(2,1)S(1)} collective-permute-done((bf16[16,16,130]{2,1,0:T(8,128)(2,1)S(1)}, bf16[16,16,130]{2,1,0:T(8,128)(2,1)S(1)}, u32[]{:S(2)}, u32[]{:S(2)}) %collective-permute-start.21) | collective-permute-done | bytes 66592 | tf_op jit(solution)/shard_map/ppermute | solution.py:27
  154.2 2.2 %collective-permute-start.14 = (bf16[1,512,256]{2,1,0:T(8,128)(2,1)}, bf16[1,512,256]{2,1,0:T(8,128)(2,1)S(1)}, u32[]{:S(2)}, u32[]{:S(2)}) collective-permute-start(bf16[1,512,256]{2,1,0:T(8,128)(2,1)} %copy-done.7), channel_id=1, source_target_pairs={{0,6},{1,7},{2,4},{3,5},{4,2},{5,3},{6,0},{7,1},{8,14},{9,15},{10,... | collective-permute-start | bytes 786440 | tf_op jit(solution)/shard_map/ppermute | solution.py:27
  157.7 5.8 %collective-permute-done.14.refs_2_ = bf16[1,512,256]{2,1,0:T(8,128)(2,1)S(1)} collective-permute-done((bf16[1,512,256]{2,1,0:T(8,128)(2,1)}, bf16[1,512,256]{2,1,0:T(8,128)(2,1)S(1)}, u32[]{:S(2)}, u32[]{:S(2)}) %collective-permute-start.14) | collective-permute-done | bytes 262176 | tf_op jit(solution)/shard_map/ppermute | solution.py:27
  164.2 2.2 %shard_map.99 = bf16[1,512,2048]{2,1,0:T(8,128)(2,1)} custom-call(s32[2]{0:T(128)S(1)} %pad_add_fusion.table, bf16[1,512,256]{2,1,0:T(8,128)(2,1)S(1)} %get-tuple-element.18.refs_0_, bf16[2,512,256]{2,1,0:T(8,128)(2,1)S(1)} %collective-permute-done.12.refs_1_, bf16[1,512,256]{2,1,0:T(8,128)(2,1)S(1)} %collective-permute-done.14.refs_2_, ...), custom_call_target="tpu_custom_call" | custom-call | flops 2097152 | bytes 4194304 | tf_op jit(solution)/shard_map/pallas_call | solution.py:238
  (114 shorter events, 24.6 us)
Async XLA Ops:
  2.4 6.6 %copy-start.10 = (bf16[16,2048]{1,0:T(8,128)(2,1)S(1)}, bf16[16,2048]{1,0:T(8,128)(2,1)}, u32[]{:S(2)}) copy-start(bf16[16,2048]{1,0:T(8,128)(2,1)} %param.11) | copy-start | bytes 196612
  3.3 16.6 %copy-start.14 = (s32[256]{0:T(256)S(1)}, s32[256]{0:T(256)}, u32[]{:S(2)}) copy-start(s32[256]{0:T(256)} %param.14) | copy-start | bytes 3076
  3.3 16.7 %copy-start.1 = (bf16[1,512,2048]{2,1,0:T(8,128)(2,1)S(1)}, bf16[1,512,2048]{2,1,0:T(8,128)(2,1)}, u32[]{:S(2)}) copy-start(bf16[1,512,2048]{2,1,0:T(8,128)(2,1)} %param.8) | copy-start | bytes 6291460
  4.2 22.4 %collective-permute-start = (bf16[2,512,256]{2,1,0:T(8,128)(2,1)}, bf16[2,512,256]{2,1,0:T(8,128)(2,1)S(1)}, u32[]{:S(2)}, u32[]{:S(2)}) collective-permute-start(bf16[2,512,256]{2,1,0:T(8,128)(2,1)} %pad_maximum_fusion.1), channel_id=1, source_target_pairs={{0,2},{1,3},{2,0},{3,1},{4,6},{5,7},{6,4},{7,5},{8,10},{9,11},{10,... | collective-permute-start | bytes 1572872 | tf_op jit(solution)/shard_map/ppermute | solution.py:27
  6.6 22.8 %collective-permute-start.2 = (bf16[2,512,256]{2,1,0:T(8,128)(2,1)}, bf16[2,512,256]{2,1,0:T(8,128)(2,1)S(1)}, u32[]{:S(2)}, u32[]{:S(2)}) collective-permute-start(bf16[2,512,256]{2,1,0:T(8,128)(2,1)} %pad_maximum_fusion.3), channel_id=1, source_target_pairs={{0,6},{1,7},{2,4},{3,5},{4,2},{5,3},{6,0},{7,1},{8,14},{9,15},{10,... | collective-permute-start | bytes 1572872 | tf_op jit(solution)/shard_map/ppermute | solution.py:27
  10.9 14.7 %all-to-all-start = ((bf16[16,2,1024]{2,1,0:T(2,128)(2,1)}), bf16[16,2,1024]{2,1,0:T(2,128)(2,1)}, u32[]{:S(2)}, u32[]{:S(2)}) async-start(bf16[16,2,1024]{2,1,0:T(2,128)(2,1)} %reshape.121), calls=%async_computation | async-start | bytes 131072 | tf_op jit(solution)/shard_map/all_to_all | solution.py:31
  28.4 35.3 %collective-permute-start.1 = (bf16[2,512,256]{2,1,0:T(8,128)(2,1)}, bf16[2,512,256]{2,1,0:T(8,128)(2,1)}, u32[]{:S(2)}, u32[]{:S(2)}) collective-permute-start(bf16[2,512,256]{2,1,0:T(8,128)(2,1)} %pad_maximum_fusion.2), channel_id=1, source_target_pairs={{0,6},{1,7},{2,4},{3,5},{4,2},{5,3},{6,0},{7,1},{8,14},{9,15},{10,... | collective-permute-start | bytes 1572872 | tf_op jit(solution)/shard_map/ppermute | solution.py:27
  29.4 60.9 %copy-start.3 = (bf16[2,512,256]{2,1,0:T(8,128)(2,1)}, bf16[2,512,256]{2,1,0:T(8,128)(2,1)S(1)}, u32[]{:S(2)}) copy-start(bf16[2,512,256]{2,1,0:T(8,128)(2,1)S(1)} %collective-permute-done.2.refs_3_) | copy-start | bytes 1572868
  30.4 33.3 %collective-permute-start.3 = (bf16[2,512,256]{2,1,0:T(8,128)(2,1)}, bf16[2,512,256]{2,1,0:T(8,128)(2,1)}, u32[]{:S(2)}, u32[]{:S(2)}) collective-permute-start(bf16[2,512,256]{2,1,0:T(8,128)(2,1)} %pad_maximum_fusion.4), channel_id=1, source_target_pairs={{0,2},{1,3},{2,0},{3,1},{4,6},{5,7},{6,4},{7,5},{8,10},{9,11},{10,... | collective-permute-start | bytes 1572872 | tf_op jit(solution)/shard_map/ppermute | solution.py:27
  32.3 33.7 %collective-permute-start.8 = (bf16[2,512,256]{2,1,0:T(8,128)(2,1)}, bf16[2,512,256]{2,1,0:T(8,128)(2,1)}, u32[]{:S(2)}, u32[]{:S(2)}) collective-permute-start(bf16[2,512,256]{2,1,0:T(8,128)(2,1)} %pad_maximum_fusion.6), channel_id=1, source_target_pairs={{0,2},{1,3},{2,0},{3,1},{4,6},{5,7},{6,4},{7,5},{8,10},{9,11},{10,... | collective-permute-start | bytes 1572872 | tf_op jit(solution)/shard_map/ppermute | solution.py:27
  44.4 11.1 %all-to-all-start.1 = ((bf16[16,2,1040]{2,1,0:T(2,128)(2,1)}), bf16[16,2,1040]{2,1,0:T(2,128)(2,1)S(1)}, u32[]{:S(2)}, u32[]{:S(2)}) async-start(bf16[16,2,1040]{2,1,0:T(2,128)(2,1)} %reshape.123), calls=%async_computation.1 | async-start | bytes 147456 | tf_op jit(solution)/shard_map/all_to_all | solution.py:31
  49.2 14.4 %copy-start = (bf16[1,2,512,1024]{3,2,1,0:T(8,128)(2,1)S(1)}, bf16[1,2,512,1024]{3,2,1,0:T(8,128)(2,1)}, u32[]{:S(2)}) copy-start(bf16[1,2,512,1024]{3,2,1,0:T(8,128)(2,1)} %param.9) | copy-start | bytes 6291460
  51.3 10.0 %collective-permute-start.5 = (bf16[2,512,256]{2,1,0:T(8,128)(2,1)}, bf16[2,512,256]{2,1,0:T(8,128)(2,1)}, u32[]{:S(2)}, u32[]{:S(2)}) collective-permute-start(bf16[2,512,256]{2,1,0:T(8,128)(2,1)} %pad_maximum_fusion.5), channel_id=1, source_target_pairs={{0,1},{1,0},{2,3},{3,2},{4,5},{5,4},{6,7},{7,6},{8,9},{9,8},{10,11... | collective-permute-start | bytes 1572872 | tf_op jit(solution)/shard_map/ppermute | solution.py:27
  59.4 1.4 collective-permute-start.7
  60.8 7.3 %collective-permute-start.10 = (bf16[2,512,256]{2,1,0:T(8,128)(2,1)S(1)}, bf16[2,512,256]{2,1,0:T(8,128)(2,1)S(1)}, u32[]{:S(2)}, u32[]{:S(2)}) collective-permute-start(bf16[2,512,256]{2,1,0:T(8,128)(2,1)S(1)} %pad_maximum_fusion.8), channel_id=1, source_target_pairs={{0,1},{1,0},{2,3},{3,2},{4,5},{5,4},{6,7},{7,6},{8,9},{9,8},{10,11... | collective-permute-start | bytes 1572872 | tf_op jit(solution)/shard_map/ppermute | solution.py:27
  61.3 16.3 %collective-permute-start.6 = (bf16[2,512,256]{2,1,0:T(8,128)(2,1)}, bf16[2,512,256]{2,1,0:T(8,128)(2,1)S(1)}, u32[]{:S(2)}, u32[]{:S(2)}) collective-permute-start(bf16[2,512,256]{2,1,0:T(8,128)(2,1)} %collective-permute-done.5), channel_id=1, source_target_pairs={{0,6},{1,7},{2,4},{3,5},{4,2},{5,3},{6,0},{7,1},{8,14},{9,15},{10,... | collective-permute-start | bytes 1572872 | tf_op jit(solution)/shard_map/ppermute | solution.py:27
  65.5 22.6 %collective-permute-start.4 = (bf16[8,512,128]{2,1,0:T(8,128)(2,1)S(1)}, bf16[8,512,128]{2,1,0:T(8,128)(2,1)S(1)}, u32[]{:S(2)}, u32[]{:S(2)}) collective-permute-start(bf16[8,512,128]{2,1,0:T(8,128)(2,1)S(1)} %shard_map.95), channel_id=1, source_target_pairs={{0,1},{1,0},{2,3},{3,2},{4,5},{5,4},{6,7},{7,6},{8,9},{9,8},{10,11... | collective-permute-start | bytes 3145736 | tf_op jit(solution)/shard_map/ppermute | solution.py:27
  65.8 12.1 %collective-permute-start.13 = (bf16[16,16,130]{2,1,0:T(8,128)(2,1)S(1)}, bf16[16,16,130]{2,1,0:T(8,128)(2,1)S(1)}, u32[]{:S(2)}, u32[]{:S(2)}) collective-permute-start(bf16[16,16,130]{2,1,0:T(8,128)(2,1)S(1)} %get-tuple-element.39.refs_8_), channel_id=1, source_target_pairs={{0,2},{1,3},{2,0},{3,1},{4,6},{5,7},{6,4},{7,5},{8,10},{9,11},{10,... | collective-permute-start | bytes 199688 | tf_op jit(solution)/shard_map/ppermute | solution.py:27
  67.0 21.1 %collective-permute-start.9 = (bf16[2,512,256]{2,1,0:T(8,128)(2,1)S(1)}, bf16[2,512,256]{2,1,0:T(8,128)(2,1)S(1)}, u32[]{:S(2)}, u32[]{:S(2)}) collective-permute-start(bf16[2,512,256]{2,1,0:T(8,128)(2,1)S(1)} %pad_maximum_fusion.7), channel_id=1, source_target_pairs={{0,6},{1,7},{2,4},{3,5},{4,2},{5,3},{6,0},{7,1},{8,14},{9,15},{10,... | collective-permute-start | bytes 1572872 | tf_op jit(solution)/shard_map/ppermute | solution.py:27
  77.6 12.7 %collective-permute-start.11 = (bf16[2,512,256]{2,1,0:T(8,128)(2,1)S(1)}, bf16[2,512,256]{2,1,0:T(8,128)(2,1)S(1)}, u32[]{:S(2)}, u32[]{:S(2)}) collective-permute-start(bf16[2,512,256]{2,1,0:T(8,128)(2,1)S(1)} %pad_maximum_fusion.9), channel_id=1, source_target_pairs={{0,2},{1,3},{2,0},{3,1},{4,6},{5,7},{6,4},{7,5},{8,10},{9,11},{10,... | collective-permute-start | bytes 1572872 | tf_op jit(solution)/shard_map/ppermute | solution.py:27
  78.3 34.0 %copy-start.2 = (bf16[1,512,2048]{2,1,0:T(8,128)(2,1)S(1)}, bf16[1,512,2048]{2,1,0:T(8,128)(2,1)}, u32[]{:S(2)}) copy-start(bf16[1,512,2048]{2,1,0:T(8,128)(2,1)} %param.8) | copy-start | bytes 6291460
  109.9 14.3 %copy-start.5 = (bf16[1,512,256]{2,1,0:T(8,128)(2,1)}, bf16[1,512,256]{2,1,0:T(8,128)(2,1)S(1)}, u32[]{:S(2)}) copy-start(bf16[1,512,256]{2,1,0:T(8,128)(2,1)S(1)} %get-tuple-element.22) | copy-start | bytes 786436
  109.9 16.6 %collective-permute-start.18 = (bf16[1,512,256]{2,1,0:T(8,128)(2,1)S(1)}, bf16[1,512,256]{2,1,0:T(8,128)(2,1)S(1)}, u32[]{:S(2)}, u32[]{:S(2)}) collective-permute-start(bf16[1,512,256]{2,1,0:T(8,128)(2,1)S(1)} %get-tuple-element.25), channel_id=1, source_target_pairs={{0,2},{1,3},{2,0},{3,1},{4,6},{5,7},{6,4},{7,5},{8,10},{9,11},{10,... | collective-permute-start | bytes 786440 | tf_op jit(solution)/shard_map/ppermute | solution.py:27
  110.4 29.5 %collective-permute-start.12 = (bf16[2,512,256]{2,1,0:T(8,128)(2,1)S(1)}, bf16[2,512,256]{2,1,0:T(8,128)(2,1)S(1)}, u32[]{:S(2)}, u32[]{:S(2)}) collective-permute-start(bf16[2,512,256]{2,1,0:T(8,128)(2,1)S(1)} %get-tuple-element.19), channel_id=1, source_target_pairs={{0,2},{1,3},{2,0},{3,1},{4,6},{5,7},{6,4},{7,5},{8,10},{9,11},{10,... | collective-permute-start | bytes 1572872 | tf_op jit(solution)/shard_map/ppermute | solution.py:27
  124.2 15.7 %collective-permute-start.17 = (bf16[1,512,256]{2,1,0:T(8,128)(2,1)S(1)}, bf16[1,512,256]{2,1,0:T(8,128)(2,1)S(1)}, u32[]{:S(2)}, u32[]{:S(2)}) collective-permute-start(bf16[1,512,256]{2,1,0:T(8,128)(2,1)S(1)} %get-tuple-element.24), channel_id=1, source_target_pairs={{0,6},{1,7},{2,4},{3,5},{4,2},{5,3},{6,0},{7,1},{8,14},{9,15},{10,... | collective-permute-start | bytes 786440 | tf_op jit(solution)/shard_map/ppermute | solution.py:27
  126.4 13.5 %collective-permute-start.19 = (bf16[1,512,256]{2,1,0:T(8,128)(2,1)S(1)}, bf16[1,512,256]{2,1,0:T(8,128)(2,1)S(1)}, u32[]{:S(2)}, u32[]{:S(2)}) collective-permute-start(bf16[1,512,256]{2,1,0:T(8,128)(2,1)S(1)} %collective-permute-done.18), channel_id=1, source_target_pairs={{0,6},{1,7},{2,4},{3,5},{4,2},{5,3},{6,0},{7,1},{8,14},{9,15},{10,... | collective-permute-start | bytes 786440 | tf_op jit(solution)/shard_map/ppermute | solution.py:27
  139.9 16.5 %copy-start.8 = (f32[16,16,130]{2,1,0:T(8,128)S(1)}, f32[16,16,130]{2,1,0:T(8,128)}, u32[]{:S(2)}) copy-start(f32[16,16,130]{2,1,0:T(8,128)} %get-tuple-element.35) | copy-start | bytes 399364
  141.1 23.2 %collective-permute-start.20 = (bf16[4,512,256]{2,1,0:T(8,128)(2,1)}, bf16[4,512,256]{2,1,0:T(8,128)(2,1)S(1)}, u32[]{:S(2)}, u32[]{:S(2)}) collective-permute-start(bf16[4,512,256]{2,1,0:T(8,128)(2,1)} %pad_maximum_fusion), channel_id=1, source_target_pairs={{0,1},{1,0},{2,3},{3,2},{4,5},{5,4},{6,7},{7,6},{8,9},{9,8},{10,11... | collective-permute-start | bytes 3145736 | tf_op jit(solution)/shard_map/ppermute | solution.py:27
  141.3 15.1 %collective-permute-start.15 = (bf16[1,512,256]{2,1,0:T(8,128)(2,1)S(1)}, bf16[1,512,256]{2,1,0:T(8,128)(2,1)}, u32[]{:S(2)}, u32[]{:S(2)}) collective-permute-start(bf16[1,512,256]{2,1,0:T(8,128)(2,1)S(1)} %copy-done.6), channel_id=1, source_target_pairs={{0,6},{1,7},{2,4},{3,5},{4,2},{5,3},{6,0},{7,1},{8,14},{9,15},{10,... | collective-permute-start | bytes 786440 | tf_op jit(solution)/shard_map/ppermute | solution.py:27
  143.9 10.2 %collective-permute-start.21 = (bf16[16,16,130]{2,1,0:T(8,128)(2,1)S(1)}, bf16[16,16,130]{2,1,0:T(8,128)(2,1)S(1)}, u32[]{:S(2)}, u32[]{:S(2)}) collective-permute-start(bf16[16,16,130]{2,1,0:T(8,128)(2,1)S(1)} %get-tuple-element.36.refs_8_), channel_id=1, source_target_pairs={{0,6},{1,7},{2,4},{3,5},{4,2},{5,3},{6,0},{7,1},{8,14},{9,15},{10,... | collective-permute-start | bytes 199688 | tf_op jit(solution)/shard_map/ppermute | solution.py:27
  154.2 9.4 %collective-permute-start.14 = (bf16[1,512,256]{2,1,0:T(8,128)(2,1)}, bf16[1,512,256]{2,1,0:T(8,128)(2,1)S(1)}, u32[]{:S(2)}, u32[]{:S(2)}) collective-permute-start(bf16[1,512,256]{2,1,0:T(8,128)(2,1)} %copy-done.7), channel_id=1, source_target_pairs={{0,6},{1,7},{2,4},{3,5},{4,2},{5,3},{6,0},{7,1},{8,14},{9,15},{10,... | collective-permute-start | bytes 786440 | tf_op jit(solution)/shard_map/ppermute | solution.py:27
  156.4 7.8 %collective-permute-start.16 = (bf16[1,512,256]{2,1,0:T(8,128)(2,1)}, bf16[1,512,256]{2,1,0:T(8,128)(2,1)S(1)}, u32[]{:S(2)}, u32[]{:S(2)}) collective-permute-start(bf16[1,512,256]{2,1,0:T(8,128)(2,1)} %collective-permute-done.15), channel_id=1, source_target_pairs={{0,2},{1,3},{2,0},{3,1},{4,6},{5,7},{6,4},{7,5},{8,10},{9,11},{10,... | collective-permute-start | bytes 786440 | tf_op jit(solution)/shard_map/ppermute | solution.py:27
  (7 other events, 15.9 us)
where the time goes:
time: 167 us
  Pallas kernels  52.6 us (31%)
  waiting for transfers between devices  45.7 us (27%)
  starting transfers between devices  35.3 us (21%)
  other arithmetic  14.8 us (9%)
  local copies, waits for them, and re-layouts  14.4 us (9%)
  between operations  2 us (1%)
  matrix products  1.9 us (1%)
    pallas_call x3, Pallas kernels, attend_call(): pl.pallas_call(kernel, grid_spec=pltpu.PrefetchScalarGridSpec(num_scalar_...  41.9 us
    ppermute x22, waiting for transfers between devices, swap(): return lax.ppermute(array, 'ctx', [(i, i ^ flip) for i in range(8)])  37.2 us
    ppermute x22, starting transfers between devices, swap(): return lax.ppermute(array, 'ctx', [(i, i ^ flip) for i in range(8)])  22.2 us
    all_to_all x2, starting transfers between devices, exchange(): return lax.all_to_all(array, 'rep', split_axis=0, concat_axis=0, tiled=True)  13.2 us
    all_to_all x2, waiting for transfers between devices, exchange(): return lax.all_to_all(array, 'rep', split_axis=0, concat_axis=0, tiled=True)  8.42 us
    pallas_call x1, Pallas kernels, over_cache(): pl.pallas_call(cache_kernel, grid_spec=pltpu.PrefetchScalarGridSpec(num_s...  6.6 us
    unnamed x37, local copies, waits for them, and re-layouts  5.54 us
    pallas_call x2, Pallas kernels, collect(): pl.pallas_call(functools.partial(collect_kernel, outs=outs, count_in=len(...  4.02 us
  transfers between devices with their start and end apart: 24, of which 9 were waited for; matrix products, arithmetic and copies ran while one was open for 15% of the time, Pallas kernels for 18%

commit v1 on v0

--- a/solution.py
+++ b/solution.py
@@ -17,7 +17,7 @@
 MASKED = -1e30
 TILE = 128
 CHUNK = 1024
-VMEM = 63_000_000
+VMEM = 54_000_000
 SMALL = 20_000_000
 BF16 = jnp.bfloat16
 F32 = jnp.float32
@@ -29,10 +29,6 @@
 
 def exchange(array):
     return lax.all_to_all(array, "rep", split_axis=0, concat_axis=0, tiled=True)
-
-
-def lanes(array, at, width):
-    return lax.dynamic_slice_in_dim(array, at * width, width, axis=array.ndim - 1)
 
 
 def attend_kernel(table, *refs, key_pieces, value_pieces, query_pieces, blocks, out_sizes, count_in):
@@ -112,13 +108,11 @@
                             weight = jnp.exp2((score - new_top) * EXP2_SCALE).astype(BF16)
                             acc[g, rows] = jnp.dot(weight, value, preferred_element_type=F32)
 
-            def full(step, unused):
-                at = pl.multiple_of((step // halves) * CHUNK, CHUNK)
-                half = (step % halves) * (512 // halves)
-                key = keys[pl.ds(at, CHUNK)]
-                value = values[pl.ds(at, CHUNK)]
-                for t in range(512 // TILE // halves):
-                    rows = pl.ds(pl.multiple_of(half + t * TILE, TILE), TILE)
+            def full(at, chunk, rows_at, count):
+                key = keys[pl.ds(at, chunk)]
+                value = values[pl.ds(at, chunk)]
+                for t in range(count):
+                    rows = pl.ds(pl.multiple_of(rows_at + t * TILE, TILE), TILE)
                     for g in range(2):
                         query = queries[n, rows, g * HD : (g + 1) * HD]
                         score = lax.dot_general(
@@ -132,9 +126,20 @@
                         more = jnp.dot(weight, value, preferred_element_type=F32)
                         acc[g, rows, :HD] = acc[g, rows, :HD] * factor + more[:, :HD]
                         acc[g, rows, HD:] = acc[g, rows, HD:] * factor + more[:, HD:]
+
+            chunks = first // CHUNK
+
+            def single(step, unused):
+                at = pl.multiple_of((chunks - 1) * CHUNK, CHUNK)
+                full(at, CHUNK, step * (512 // halves), 512 // TILE // halves)
                 return unused
 
-            lax.fori_loop(0, (first // CHUNK) * halves, full, 0)
+            def double(step, unused):
+                full(pl.multiple_of(step * 2 * CHUNK, 2 * CHUNK), 2 * CHUNK, 0, 512 // TILE)
+                return unused
+
+            lax.fori_loop(0, (chunks % 2) * halves, single, 0)
+            lax.fori_loop(0, chunks // 2, double, 0)
             live = lax.broadcasted_iota(jnp.int32, (512, HD), 0) + first < valid
             for g in range(2):
                 mixed = acc[g, :, :HD] / acc[g, :, HD:]
@@ -153,11 +158,15 @@
         for more in range(1, len(blocks)):
             flip = jnp.where(n == more, blocks[more], flip)
         one_block(n, me ^ flip)
+        for at, copy in enumerate(leaving):
+
+            @pl.when(n == at)
+            def _(copy=copy):
+                copy.start()
+
         return unused
 
     lax.fori_loop(0, len(blocks), step, 0)
-    for copy in leaving:
-        copy.start()
     for copy in leaving:
         copy.wait()
     token[...] = jnp.zeros_like(token)
@@ -257,31 +266,32 @@
     return lax.optimization_barrier((value, *others))[0]
 
 
-def wide(array, at):
-    return lanes(array, at, 2 * HD)
-
-
-def prefill_pairs(me, pre_pairs):
+def wide(query, at):
+    return lax.dynamic_slice(query, (0, 0, at * 2 * HD), (1, 512, 2 * HD))
+
+
+def wide_pairs(pairs, index, at):
+    return lax.dynamic_slice(pairs, (0, index, 0, at * 2 * HD), (1, 1, 512, 2 * HD))[0]
+
+
+def prefill_pairs(me, pairs):
     chip = me >> 1
-    key, value = pre_pairs[0, 0], pre_pairs[0, 1]
-    key_1 = jnp.stack([wide(key, chip ^ 1), wide(key, chip ^ 2)])
-    value_1 = jnp.stack([wide(value, chip ^ 3), wide(value, chip ^ 2)])
+    key_1 = jnp.concatenate([wide_pairs(pairs, 0, chip ^ 1), wide_pairs(pairs, 0, chip ^ 2)])
+    value_1 = jnp.concatenate([wide_pairs(pairs, 1, chip ^ 3), wide_pairs(pairs, 1, chip ^ 2)])
     return key_1, value_1
 
 
-def prefill_pairs_on(me, pre_pairs, key_1, value_1):
+def prefill_pairs_on(me, pairs, key_1, value_1):
     chip = me >> 1
-    key, value = pre_pairs[0, 0], pre_pairs[0, 1]
-    key_2 = jnp.stack([wide(key, chip ^ 3), key_1[1]])
-    value_2 = jnp.stack([wide(value, chip ^ 1), value_1[1]])
+    key_2 = jnp.concatenate([wide_pairs(pairs, 0, chip ^ 3), key_1[1:2]])
+    value_2 = jnp.concatenate([wide_pairs(pairs, 1, chip ^ 1), value_1[1:2]])
     return key_2, value_2
 
 
 def prefill_queries(me, query):
-    query_x = swap(jnp.stack([wide(query, me ^ 7), wide(query, me ^ 5)]), 1)
-    query_y = swap(jnp.stack([wide(query, me ^ 1), wide(query, me ^ 3)]), 1)
-    query_a1 = jnp.stack([wide(query, me ^ 2), wide(query, me ^ 4)])
-    return query_x, query_y, query_a1
+    query_x = swap(jnp.concatenate([wide(query, me ^ 7), wide(query, me ^ 5)]), 1)
+    query_a1 = jnp.concatenate([wide(query, me ^ 2), wide(query, me ^ 4)])
+    return query_x, query_a1
 
 
 def prefill_across(table, pairs, key_1, key_2, value_1, value_2):
@@ -491,36 +501,37 @@
     table = jnp.stack([me, prefill_len[0]]).astype(jnp.int32)
     pairs, query = pre_pairs[0], pre_query[0]
     key_1, value_1 = prefill_pairs(me, pre_pairs)
+    query_later = after(pre_query, key_1, value_1)
+    key_1, value_1 = swap(key_1, 2), swap(value_1, 6)
+    query_b1, query_a1 = prefill_queries(me, query_later)
     dest_rep, lengths, source_rep = decode_tables(cache, cached_len, move)
-    outgoing = after(decode_send(source_rep, dec_query), key_1, value_1)
-    key_1, value_1 = swap(key_1, 2), swap(value_1, 6)
+    outgoing = after(decode_send(source_rep, dec_query), query_a1)
+    query_a1, query_b1 = swap(query_a1, 2), swap(query_b1, 6)
     arrived = exchange(outgoing)
     key_2, value_2 = prefill_pairs_on(me, pre_pairs, key_1, value_1)
-    query_later = after(query, outgoing, key_2, value_2)
+    query_later = after(pre_query, outgoing, key_2, value_2)
     key_2, value_2 = swap(key_2, 6), swap(value_2, 2)
-    query_b1, query_x, query_a1 = prefill_queries(me, query_later)
-    arrived = after(arrived, query_a1)
-    query_a1, query_b1 = swap(query_a1, 2), swap(query_b1, 6)
+    query_x = jnp.concatenate([wide(query_later, me ^ 1), wide(query_later, me ^ 3)])
+    arrived = after(arrived, query_x)
+    query_x = swap(query_x, 1)
     partial = decode_home(me, lengths, dest_rep, arrived, cache)
     back = exchange(partial)
     pairs_x = prefill_across(table, pairs, key_1, key_2, value_1, value_2)
     keyed = [pairs, key_1, key_2, value_1, value_2, pairs_x]
-    query_a2 = swap(jnp.stack([wide(query, me ^ 6), query_a1[1]]), 6)
-    query_b2 = swap(jnp.stack([query_x[1], query_b1[1]]), 2)
-    back = decode_order(source_rep, back)
-    other = swap(back, 1)
+    query_a2 = swap(jnp.concatenate([wide(pre_query, me ^ 6), query_a1[1:2]]), 6)
+    query_b2 = swap(jnp.concatenate([query_x[1:2], query_b1[1:2]]), 2)
     out_5, out_4, out_32, token = part(
         table,
         keyed,
-        [query_a1, query_a2, query_b2, back],
+        [query_a1, query_a2, query_b2, partial],
         [(8, 1, None), (7, 1, None), (8, 0, None), (6, 0, None)],
         [5, 4, 3, 2],
         [1, 1, 2],
     )
     back_5, back_4 = swap(out_5, 2), swap(out_4, 6)
     back_32 = swap(out_32, 2)
-    back = packed(*merge(back, other))
-    other = swap(back, 2)
+    back = decode_order(source_rep, after(back, token))
+    other = swap(back, 6)
     out_0, out_7, token = part(
         table,
         keyed,
@@ -533,11 +544,13 @@
     back_4 = swap(back_4, 2)
     back_7 = swap(out_7, 6)
     back = packed(*merge(back, other))
-    other = swap(back, 6)
+    other = swap(back, 2)
     out_1, out_6, token = part(
         table, keyed, [query_a2, query_x, back, token], [(7, 0, None), (6, 0, None)], [1, 6], [1, 1]
     )
     back_6 = swap(out_6, 6)
+    back = packed(*merge(back, after(other, token)))
+    other = swap(back, 1)
     back_x = swap(jnp.concatenate([out_1, back_32[0:1], back_7, back_5]), 1)
     pre_out = prefill_join(table, [out_0, back_32, back_6, back_4, back_x])
     weighted, top, total = merge(back, other)

time: 167 us -> 154 us (0.922)
  waiting for transfers between devices: 45.7 us -> 25.9 us
  local copies, waits for them, and re-layouts: 14.4 us -> 20.5 us
  other arithmetic: 14.8 us -> 16.5 us
    ppermute x22, waiting for transfers between devices: 37.2 us -> 20.9 us  [swap(): return lax.ppermute(array, 'ctx', [(i, i ^ flip) for i in range(8)])]
    concatenate x0 -> x9, other arithmetic: none -> 8.63 us  [the longest x1 1.79 us: prefill_pairs_on(): key_2 = jnp.concatenate([wide_pairs(pairs, 0, chip ^ 3), key_1[1:2]])]
    another operation x13 -> x4, other arithmetic: 8.96 us -> 0.56 us  [the longest x1 2.03 us: prefill_queries(): query_x = swap(jnp.stack([wide(query, me ^ 7), wide(query, me ^ 5)]), 1)]
    unnamed x37 -> x42, local copies, waits for them, and re-layouts: 5.54 us -> 9.8 us
    all_to_all x2, waiting for transfers between devices: 8.42 us -> 4.99 us  [exchange(): return lax.all_to_all(array, 'rep', split_axis=0, concat_axis=0, tiled=True)]
    all_to_all x2, starting transfers between devices: 13.2 us -> 15.5 us  [exchange(): return lax.all_to_all(array, 'rep', split_axis=0, concat_axis=0, tiled=True)]
    squeeze x0 -> x1, local copies, waits for them, and re-layouts: none -> 2.34 us  [wide_pairs(): lax.dynamic_slice(pairs, (0, index, 0, at * 2 * HD), (1, 1, 512, 2 * HD))[0]]
    another operation x2 -> x0, local copies, waits for them, and re-layouts: 1.91 us -> none  [the longest x1 1 us: prefill_queries(): query_y = swap(jnp.stack([wide(query, me ^ 1), wide(query, me ^ 3)]), 1)]
  transfers between devices with their start and end apart: 24 -> 24, of which waited for: 9 -> 6; matrix products, arithmetic and copies ran while one was open for 15% -> 19% of each run, Pallas kernels for 18% -> 20%
where the time goes in v1:
time: 154 us; the launch traced here: 153 us
  Pallas kernels  51.4 us (33%)
  starting transfers between devices  36.6 us (24%)
  waiting for transfers between devices  25.9 us (17%)
  local copies, waits for them, and re-layouts  20.5 us (13%)
  other arithmetic  16.5 us (11%)
  between operations  1.95 us (1%)
    pallas_call x3, Pallas kernels, attend_call(): pl.pallas_call(kernel, grid_spec=pltpu.PrefetchScalarGridSpec(num_scalar_...  40.6 us
    ppermute x22, starting transfers between devices, swap(): return lax.ppermute(array, 'ctx', [(i, i ^ flip) for i in range(8)])  21.1 us
    ppermute x22, waiting for transfers between devices, swap(): return lax.ppermute(array, 'ctx', [(i, i ^ flip) for i in range(8)])  20.9 us
    all_to_all x2, starting transfers between devices, exchange(): return lax.all_to_all(array, 'rep', split_axis=0, concat_axis=0, tiled=True)  15.5 us
    unnamed x42, local copies, waits for them, and re-layouts  9.8 us
    pallas_call x1, Pallas kernels, over_cache(): pl.pallas_call(cache_kernel, grid_spec=pltpu.PrefetchScalarGridSpec(num_s...  5.82 us
    all_to_all x2, waiting for transfers between devices, exchange(): return lax.all_to_all(array, 'rep', split_axis=0, concat_axis=0, tiled=True)  4.99 us
    pallas_call x2, Pallas kernels, collect(): pl.pallas_call(functools.partial(collect_kernel, outs=outs, count_in=len(...  4.99 us
  transfers between devices with their start and end apart: 24, of which 6 were waited for; matrix products, arithmetic and copies ran while one was open for 19% of the time, Pallas kernels for 20%

profile of v1, /device:TPU:2, one launch (start us, length us, event | category | flops | bytes accessed | tf_op | source)
XLA Modules:
  0.0 153.3 jit_solution(8082378920399257560)
XLA Ops:
  0.7 2.3 %dynamic-slice_bitcast_fusion = (bf16[1,512,256]{2,1,0:T(8,128)(2,1)S(1)}, bf16[1,512,256]{2,1,0:T(8,128)(2,1)S(1)}, bf16[1,512,256]{2,1,0:T(8,128)(2,1)}, bf16[...) fusion(bf16[1,2,512,1024]{3,2,1,0:T(8,128)(2,1)} %param.9, ...), kind=kLoop, calls=%fused_computation.12 | loop fusion | bytes 3145740 | tf_op jit(solution)/shard_map/squeeze | solution.py:274
  3.8 1.6 %collective-permute-start = (bf16[2,512,256]{2,1,0:T(8,128)(2,1)}, bf16[2,512,256]{2,1,0:T(8,128)(2,1)S(1)}, u32[]{:S(2)}, u32[]{:S(2)}) collective-permute-start(bf16[2,512,256]{2,1,0:T(8,128)(2,1)} %pad_maximum_fusion.1), channel_id=1, source_target_pairs={{0,2},{1,3},{2,0},{3,1},{4,6},{5,7},{6,4},{7,5},{8,10},{9,11},{10,... | collective-permute-start | bytes 1572872 | tf_op jit(solution)/shard_map/ppermute | solution.py:27
  6.3 2.2 %collective-permute-start.2 = (bf16[2,512,256]{2,1,0:T(8,128)(2,1)}, bf16[2,512,256]{2,1,0:T(8,128)(2,1)S(1)}, u32[]{:S(2)}, u32[]{:S(2)}) collective-permute-start(bf16[2,512,256]{2,1,0:T(8,128)(2,1)} %pad_maximum_fusion.3), channel_id=1, source_target_pairs={{0,6},{1,7},{2,4},{3,5},{4,2},{5,3},{6,0},{7,1},{8,14},{9,15},{10,... | collective-permute-start | bytes 1572872 | tf_op jit(solution)/shard_map/ppermute | solution.py:27
  13.8 8.3 %all-to-all-start = ((bf16[16,2,1024]{2,1,0:T(2,128)(2,1)}), bf16[16,2,1024]{2,1,0:T(2,128)(2,1)}, u32[]{:S(2)}, u32[]{:S(2)}) async-start(bf16[16,2,1024]{2,1,0:T(2,128)(2,1)} %reshape.110), calls=%async_computation | async-start | bytes 131072 | tf_op jit(solution)/shard_map/all_to_all | solution.py:31
  25.3 1.8 %pad_maximum_fusion.2 = bf16[2,512,256]{2,1,0:T(8,128)(2,1)} fusion(bf16[1,512,256]{2,1,0:T(8,128)(2,1)S(1)} %slice.108, bf16[1,512,256]{2,1,0:T(8,128)(2,1)} %get-tuple-element.53), kind=kLoop, calls=%fused_computation.4 | loop fusion | flops 262144 | bytes 1048576 | tf_op jit(solution)/shard_map/concatenate | solution.py:286
  28.6 1.2 collective-permute-start.3
  29.7 1.1 constant_dynamic-slice_fusion.2
  31.7 2.2 %collective-permute-start.6 = (bf16[2,512,256]{2,1,0:T(8,128)(2,1)}, bf16[2,512,256]{2,1,0:T(8,128)(2,1)}, u32[]{:S(2)}, u32[]{:S(2)}) collective-permute-start(bf16[2,512,256]{2,1,0:T(8,128)(2,1)} %collective-permute-done.5), channel_id=1, source_target_pairs={{0,6},{1,7},{2,4},{3,5},{4,2},{5,3},{6,0},{7,1},{8,14},{9,15},{10,... | collective-permute-start | bytes 1572872 | tf_op jit(solution)/shard_map/ppermute | solution.py:27
  36.7 6.6 %collective-permute-done.1.refs_2_ = bf16[2,512,256]{2,1,0:T(8,128)(2,1)} collective-permute-done((bf16[2,512,256]{2,1,0:T(8,128)(2,1)}, bf16[2,512,256]{2,1,0:T(8,128)(2,1)}, u32[]{:S(2)}, u32[]{:S(2)}) %collective-permute-start.1) | collective-permute-done | bytes 524320 | tf_op jit(solution)/shard_map/ppermute | solution.py:27
  43.4 2.8 %shard_map.95 = bf16[8,512,128]{2,1,0:T(8,128)(2,1)} custom-call(s32[2]{0:T(128)S(1)} %pad_add_fusion.table, bf16[2,512,1024]{2,1,0:T(8,128)(2,1)S(1)} %bitcast.36, bf16[2,512,256]{2,1,0:T(8,128)(2,1)S(1)} %collective-permute-done.refs_1_, bf16[2,512,256]{2,1,0:T(8,128)(2,1)} %collective-permute-done.1.refs_2_, ...), custom_call_target="tpu_custom_call" | custom-call | flops 1048576 | bytes 2097152 | tf_op jit(solution)/shard_map/pallas_call | solution.py:247
  47.1 1.4 collective-permute-start.8
  48.5 6.1 %collective-permute-done.6.refs_7_ = bf16[2,512,256]{2,1,0:T(8,128)(2,1)} collective-permute-done((bf16[2,512,256]{2,1,0:T(8,128)(2,1)}, bf16[2,512,256]{2,1,0:T(8,128)(2,1)}, u32[]{:S(2)}, u32[]{:S(2)}) %collective-permute-start.6) | collective-permute-done | bytes 524320 | tf_op jit(solution)/shard_map/ppermute | solution.py:27
  57.6 5.8 %over_cache.1 = bf16[16,16,256]{2,1,0:T(8,128)(2,1)S(1)} custom-call(s32[33]{0:T(128)S(1)} %pad_add_fusion.1.table, bf16[16,16,128]{2,1,0:T(8,128)(2,1)S(1)} %bitcast.43, bf16[16,2,128,1024]{3,2,1,0:T(8,128)(2,1)} %cache_ref.1), custom_call_target="tpu_custom_call" | custom-call | flops 8000000000 | bytes 8500000 | tf_op jit(solution)/shard_map/over_cache/pallas_call | solution.py:406
  63.6 1.7 %reduce.19 = bf16[16,2080]{1,0:T(8,128)(2,1)} reduce(bf16[16,1,2080]{2,1,0:T(2,128)(2,1)S(1)} %all_to_all.22, bf16[]{:T(256)} %broadcast.99), dimensions={1}, to_apply=%all_to_all.22.reduce_sub_computation | reduce | bytes 133122 | tf_op jit(solution)/shard_map/all_to_all | solution.py:31
  65.3 1.6 %reshape.112 = bf16[16,2,1040]{2,1,0:T(2,128)(2,1)} reshape(bf16[16,2080]{1,0:T(8,128)(2,1)} %reduce.19) | data formatting | bytes 133120
  67.0 7.2 %all-to-all-start.1 = ((bf16[16,2,1040]{2,1,0:T(2,128)(2,1)}), bf16[16,2,1040]{2,1,0:T(2,128)(2,1)}, u32[]{:S(2)}, u32[]{:S(2)}) async-start(bf16[16,2,1040]{2,1,0:T(2,128)(2,1)} %reshape.112), calls=%async_computation.1 | async-start | bytes 147456 | tf_op jit(solution)/shard_map/all_to_all | solution.py:31
  74.2 1.1 multiply_reduce_fusion
  75.6 5.0 %all-to-all-done.1 = bf16[16,2,1040]{2,1,0:T(2,128)(2,1)} async-done(((bf16[16,2,1040]{2,1,0:T(2,128)(2,1)}), bf16[16,2,1040]{2,1,0:T(2,128)(2,1)}, u32[]{:S(2)}, u32[]{:S(2)}) %all-to-all-start.1) | async-done | bytes 66592 | tf_op jit(solution)/shard_map/all_to_all | solution.py:31
  81.6 19.0 %shard_map.96 = (bf16[1,512,256]{2,1,0:T(8,128)(2,1)S(1)}, bf16[1,512,256]{2,1,0:T(8,128)(2,1)S(1)}, bf16[2,512,256]{2,1,0:T(8,128)(2,1)S(1)}, f32[8,128]{1,0:T(8,128)S(1)}) custom-call(s32[2]{0:T(128)S(1)} %pad_add_fusion.table, bf16[2,512,1024]{2,1,0:T(8,128)(2,1)S(1)} %bitcast.37, bf16[2,512,256]{2,1,0:T(8,128)(2,1)S(1)} %collective-permute-done.refs_1_, ...), custom_call_target="tpu_custom_call" | custom-call | flops 4800000000 | bytes 4000000 | tf_op jit(solution)/shard_map/pallas_call | solution.py:186
  103.5 1.1 collective-permute-start.12
  105.6 2.5 %collective-permute-start.14 = (bf16[1,512,256]{2,1,0:T(8,128)(2,1)}, bf16[1,512,256]{2,1,0:T(8,128)(2,1)}, u32[]{:S(2)}, u32[]{:S(2)}) collective-permute-start(bf16[1,512,256]{2,1,0:T(8,128)(2,1)} %copy-done.6), channel_id=1, source_target_pairs={{0,6},{1,7},{2,4},{3,5},{4,2},{5,3},{6,0},{7,1},{8,14},{9,15},{10,... | collective-permute-start | bytes 786440 | tf_op jit(solution)/shard_map/ppermute | solution.py:27
  108.2 1.6 %copy-done.2 = bf16[1,512,2048]{2,1,0:T(8,128)(2,1)S(1)} copy-done((bf16[1,512,2048]{2,1,0:T(8,128)(2,1)S(1)}, bf16[1,512,2048]{2,1,0:T(8,128)(2,1)}, u32[]{:S(2)}) %copy-start.2) | copy-done | bytes 2097176
  109.8 1.0 copy-done.4
  110.9 10.5 %shard_map.97 = (bf16[1,512,256]{2,1,0:T(8,128)(2,1)S(1)}, bf16[1,512,256]{2,1,0:T(8,128)(2,1)S(1)}, f32[8,128]{1,0:T(8,128)S(1)}) custom-call(s32[2]{0:T(128)S(1)} %pad_add_fusion.table, bf16[2,512,1024]{2,1,0:T(8,128)(2,1)S(1)} %bitcast.38, bf16[2,512,256]{2,1,0:T(8,128)(2,1)S(1)} %collective-permute-done.refs_1_, ...), custom_call_target="tpu_custom_call" | custom-call | flops 2400000000 | bytes 4000000 | tf_op jit(solution)/shard_map/pallas_call | solution.py:186
  121.4 1.1 collective-permute-start.16
  123.1 1.0 collective-permute-start.20
  124.1 2.5 %collective-permute-start.18 = (bf16[1,512,256]{2,1,0:T(8,128)(2,1)S(1)}, bf16[1,512,256]{2,1,0:T(8,128)(2,1)S(1)}, u32[]{:S(2)}, u32[]{:S(2)}) collective-permute-start(bf16[1,512,256]{2,1,0:T(8,128)(2,1)S(1)} %collective-permute-done.17), channel_id=1, source_target_pairs={{0,6},{1,7},{2,4},{3,5},{4,2},{5,3},{6,0},{7,1},{8,14},{9,15},{10,... | collective-permute-start | bytes 786440 | tf_op jit(solution)/shard_map/ppermute | solution.py:27
  126.6 11.1 %shard_map.98 = (bf16[1,512,256]{2,1,0:T(8,128)(2,1)S(1)}, bf16[1,512,256]{2,1,0:T(8,128)(2,1)S(1)}, f32[8,128]{1,0:T(8,128)}) custom-call(s32[2]{0:T(128)S(1)} %pad_add_fusion.table, bf16[2,512,1024]{2,1,0:T(8,128)(2,1)S(1)} %bitcast.39, bf16[2,512,256]{2,1,0:T(8,128)(2,1)S(1)} %collective-permute-done.refs_1_, ...), custom_call_target="tpu_custom_call" | custom-call | flops 2400000000 | bytes 4000000 | tf_op jit(solution)/shard_map/pallas_call | solution.py:186
  138.0 1.1 pad_maximum_fusion
  141.1 1.1 collective-permute-done.21
  143.8 6.3 %collective-permute-done.13.refs_2_ = bf16[1,512,256]{2,1,0:T(8,128)(2,1)S(1)} collective-permute-done((bf16[1,512,256]{2,1,0:T(8,128)(2,1)}, bf16[1,512,256]{2,1,0:T(8,128)(2,1)S(1)}, u32[]{:S(2)}, u32[]{:S(2)}) %collective-permute-start.13) | collective-permute-done | bytes 262176 | tf_op jit(solution)/shard_map/ppermute | solution.py:27
  150.9 2.2 %shard_map.99 = bf16[1,512,2048]{2,1,0:T(8,128)(2,1)} custom-call(s32[2]{0:T(128)S(1)} %pad_add_fusion.table, bf16[1,512,256]{2,1,0:T(8,128)(2,1)S(1)} %get-tuple-element.22.refs_0_, bf16[2,512,256]{2,1,0:T(8,128)(2,1)S(1)} %collective-permute-done.11.refs_1_, bf16[1,512,256]{2,1,0:T(8,128)(2,1)S(1)} %collective-permute-done.13.refs_2_, ...), custom_call_target="tpu_custom_call" | custom-call | flops 2097152 | bytes 4194304 | tf_op jit(solution)/shard_map/pallas_call | solution.py:247
  (120 shorter events, 29.2 us)
Async XLA Ops:
  0.7 7.8 %copy-start.1 = (bf16[1,512,2048]{2,1,0:T(8,128)(2,1)S(1)}, bf16[1,512,2048]{2,1,0:T(8,128)(2,1)}, u32[]{:S(2)}) copy-start(bf16[1,512,2048]{2,1,0:T(8,128)(2,1)} %param.8) | copy-start | bytes 6291460
  3.8 21.4 %collective-permute-start = (bf16[2,512,256]{2,1,0:T(8,128)(2,1)}, bf16[2,512,256]{2,1,0:T(8,128)(2,1)S(1)}, u32[]{:S(2)}, u32[]{:S(2)}) collective-permute-start(bf16[2,512,256]{2,1,0:T(8,128)(2,1)} %pad_maximum_fusion.1), channel_id=1, source_target_pairs={{0,2},{1,3},{2,0},{3,1},{4,6},{5,7},{6,4},{7,5},{8,10},{9,11},{10,... | collective-permute-start | bytes 1572872 | tf_op jit(solution)/shard_map/ppermute | solution.py:27
  6.3 21.4 %collective-permute-start.2 = (bf16[2,512,256]{2,1,0:T(8,128)(2,1)}, bf16[2,512,256]{2,1,0:T(8,128)(2,1)S(1)}, u32[]{:S(2)}, u32[]{:S(2)}) collective-permute-start(bf16[2,512,256]{2,1,0:T(8,128)(2,1)} %pad_maximum_fusion.3), channel_id=1, source_target_pairs={{0,6},{1,7},{2,4},{3,5},{4,2},{5,3},{6,0},{7,1},{8,14},{9,15},{10,... | collective-permute-start | bytes 1572872 | tf_op jit(solution)/shard_map/ppermute | solution.py:27
  9.4 22.3 %collective-permute-start.5 = (bf16[2,512,256]{2,1,0:T(8,128)(2,1)}, bf16[2,512,256]{2,1,0:T(8,128)(2,1)}, u32[]{:S(2)}, u32[]{:S(2)}) collective-permute-start(bf16[2,512,256]{2,1,0:T(8,128)(2,1)} %pad_maximum_fusion.5), channel_id=1, source_target_pairs={{0,1},{1,0},{2,3},{3,2},{4,5},{5,4},{6,7},{7,6},{8,9},{9,8},{10,11... | collective-permute-start | bytes 1572872 | tf_op jit(solution)/shard_map/ppermute | solution.py:27
  10.3 25.5 %collective-permute-start.7 = (bf16[2,512,256]{2,1,0:T(8,128)(2,1)}, bf16[2,512,256]{2,1,0:T(8,128)(2,1)}, u32[]{:S(2)}, u32[]{:S(2)}) collective-permute-start(bf16[2,512,256]{2,1,0:T(8,128)(2,1)} %pad_maximum_fusion.6), channel_id=1, source_target_pairs={{0,2},{1,3},{2,0},{3,1},{4,6},{5,7},{6,4},{7,5},{8,10},{9,11},{10,... | collective-permute-start | bytes 1572872 | tf_op jit(solution)/shard_map/ppermute | solution.py:27
  11.8 15.9 %copy-start.13 = (s32[16]{0:T(128)}, s32[16]{0:T(128)S(1)}, u32[]{:S(2)}) copy-start(s32[16]{0:T(128)S(1)} %get-tuple-element.64) | copy-start | bytes 196
  13.8 21.0 %all-to-all-start = ((bf16[16,2,1024]{2,1,0:T(2,128)(2,1)}), bf16[16,2,1024]{2,1,0:T(2,128)(2,1)}, u32[]{:S(2)}, u32[]{:S(2)}) async-start(bf16[16,2,1024]{2,1,0:T(2,128)(2,1)} %reshape.110), calls=%async_computation | async-start | bytes 131072 | tf_op jit(solution)/shard_map/all_to_all | solution.py:31
  27.0 6.9 %copy-start.11 = (bf16[16,2,1024]{2,1,0:T(2,128)(2,1)S(1)}, bf16[16,2,1024]{2,1,0:T(2,128)(2,1)}, u32[]{:S(2)}) copy-start(bf16[16,2,1024]{2,1,0:T(2,128)(2,1)} %param.12) | copy-start | bytes 196612
  27.0 7.7 %copy-start.16 = (s32[16]{0:T(128)S(1)}, s32[16]{0:T(128)}, u32[]{:S(2)}) copy-start(s32[16]{0:T(128)} %get-tuple-element.63) | copy-start | bytes 196
  27.0 16.3 %collective-permute-start.1 = (bf16[2,512,256]{2,1,0:T(8,128)(2,1)}, bf16[2,512,256]{2,1,0:T(8,128)(2,1)}, u32[]{:S(2)}, u32[]{:S(2)}) collective-permute-start(bf16[2,512,256]{2,1,0:T(8,128)(2,1)} %pad_maximum_fusion.2), channel_id=1, source_target_pairs={{0,6},{1,7},{2,4},{3,5},{4,2},{5,3},{6,0},{7,1},{8,14},{9,15},{10,... | collective-permute-start | bytes 1572872 | tf_op jit(solution)/shard_map/ppermute | solution.py:27
  27.7 53.9 %copy-start.3 = (bf16[2,512,256]{2,1,0:T(8,128)(2,1)}, bf16[2,512,256]{2,1,0:T(8,128)(2,1)S(1)}, u32[]{:S(2)}) copy-start(bf16[2,512,256]{2,1,0:T(8,128)(2,1)S(1)} %collective-permute-done.2.refs_3_) | copy-start | bytes 1572868
  27.7 15.7 %copy-start = (bf16[1,2,512,1024]{3,2,1,0:T(8,128)(2,1)S(1)}, bf16[1,2,512,1024]{3,2,1,0:T(8,128)(2,1)}, u32[]{:S(2)}) copy-start(bf16[1,2,512,1024]{3,2,1,0:T(8,128)(2,1)} %param.9) | copy-start | bytes 6291460
  28.6 14.8 %collective-permute-start.3 = (bf16[2,512,256]{2,1,0:T(8,128)(2,1)}, bf16[2,512,256]{2,1,0:T(8,128)(2,1)}, u32[]{:S(2)}, u32[]{:S(2)}) collective-permute-start(bf16[2,512,256]{2,1,0:T(8,128)(2,1)} %pad_maximum_fusion.4), channel_id=1, source_target_pairs={{0,2},{1,3},{2,0},{3,1},{4,6},{5,7},{6,4},{7,5},{8,10},{9,11},{10,... | collective-permute-start | bytes 1572872 | tf_op jit(solution)/shard_map/ppermute | solution.py:27
  31.7 23.9 %collective-permute-start.9 = (bf16[2,512,256]{2,1,0:T(8,128)(2,1)}, bf16[2,512,256]{2,1,0:T(8,128)(2,1)}, u32[]{:S(2)}, u32[]{:S(2)}) collective-permute-start(bf16[2,512,256]{2,1,0:T(8,128)(2,1)} %pad_maximum_fusion.7), channel_id=1, source_target_pairs={{0,1},{1,0},{2,3},{3,2},{4,5},{5,4},{6,7},{7,6},{8,9},{9,8},{10,11... | collective-permute-start | bytes 1572872 | tf_op jit(solution)/shard_map/ppermute | solution.py:27
  31.7 22.9 %collective-permute-start.6 = (bf16[2,512,256]{2,1,0:T(8,128)(2,1)}, bf16[2,512,256]{2,1,0:T(8,128)(2,1)}, u32[]{:S(2)}, u32[]{:S(2)}) collective-permute-start(bf16[2,512,256]{2,1,0:T(8,128)(2,1)} %collective-permute-done.5), channel_id=1, source_target_pairs={{0,6},{1,7},{2,4},{3,5},{4,2},{5,3},{6,0},{7,1},{8,14},{9,15},{10,... | collective-permute-start | bytes 1572872 | tf_op jit(solution)/shard_map/ppermute | solution.py:27
  46.1 35.5 %collective-permute-start.4 = (bf16[8,512,128]{2,1,0:T(8,128)(2,1)}, bf16[8,512,128]{2,1,0:T(8,128)(2,1)}, u32[]{:S(2)}, u32[]{:S(2)}) collective-permute-start(bf16[8,512,128]{2,1,0:T(8,128)(2,1)} %shard_map.95), channel_id=1, source_target_pairs={{0,1},{1,0},{2,3},{3,2},{4,5},{5,4},{6,7},{7,6},{8,9},{9,8},{10,11... | collective-permute-start | bytes 3145736 | tf_op jit(solution)/shard_map/ppermute | solution.py:27
  47.1 34.5 %collective-permute-start.8 = (bf16[2,512,256]{2,1,0:T(8,128)(2,1)}, bf16[2,512,256]{2,1,0:T(8,128)(2,1)}, u32[]{:S(2)}, u32[]{:S(2)}) collective-permute-start(bf16[2,512,256]{2,1,0:T(8,128)(2,1)} %pad_maximum_fusion.8), channel_id=1, source_target_pairs={{0,6},{1,7},{2,4},{3,5},{4,2},{5,3},{6,0},{7,1},{8,14},{9,15},{10,... | collective-permute-start | bytes 1572872 | tf_op jit(solution)/shard_map/ppermute | solution.py:27
  57.4 24.2 %collective-permute-start.10 = (bf16[2,512,256]{2,1,0:T(8,128)(2,1)}, bf16[2,512,256]{2,1,0:T(8,128)(2,1)}, u32[]{:S(2)}, u32[]{:S(2)}) collective-permute-start(bf16[2,512,256]{2,1,0:T(8,128)(2,1)} %pad_maximum_fusion.9), channel_id=1, source_target_pairs={{0,2},{1,3},{2,0},{3,1},{4,6},{5,7},{6,4},{7,5},{8,10},{9,11},{10,... | collective-permute-start | bytes 1572872 | tf_op jit(solution)/shard_map/ppermute | solution.py:27
  67.0 13.6 %all-to-all-start.1 = ((bf16[16,2,1040]{2,1,0:T(2,128)(2,1)}), bf16[16,2,1040]{2,1,0:T(2,128)(2,1)}, u32[]{:S(2)}, u32[]{:S(2)}) async-start(bf16[16,2,1040]{2,1,0:T(2,128)(2,1)} %reshape.112), calls=%async_computation.1 | async-start | bytes 147456 | tf_op jit(solution)/shard_map/all_to_all | solution.py:31
  81.6 21.3 %copy-start.14 = (s32[16]{0:T(128)S(1)}, s32[16]{0:T(128)}, u32[]{:S(2)}) copy-start(s32[16]{0:T(128)} %copy-done.13) | copy-start | bytes 196
  103.5 19.0 %collective-permute-start.12 = (bf16[16,16,130]{2,1,0:T(8,128)(2,1)S(1)}, bf16[16,16,130]{2,1,0:T(8,128)(2,1)S(1)}, u32[]{:S(2)}, u32[]{:S(2)}) collective-permute-start(bf16[16,16,130]{2,1,0:T(8,128)(2,1)S(1)} %reshape.96.refs_8_), channel_id=1, source_target_pairs={{0,6},{1,7},{2,4},{3,5},{4,2},{5,3},{6,0},{7,1},{8,14},{9,15},{10,... | collective-permute-start | bytes 199688 | tf_op jit(solution)/shard_map/ppermute | solution.py:27
  104.6 33.3 %collective-permute-start.11 = (bf16[2,512,256]{2,1,0:T(8,128)(2,1)}, bf16[2,512,256]{2,1,0:T(8,128)(2,1)S(1)}, u32[]{:S(2)}, u32[]{:S(2)}) collective-permute-start(bf16[2,512,256]{2,1,0:T(8,128)(2,1)} %copy-done.5), channel_id=1, source_target_pairs={{0,2},{1,3},{2,0},{3,1},{4,6},{5,7},{6,4},{7,5},{8,10},{9,11},{10,... | collective-permute-start | bytes 1572872 | tf_op jit(solution)/shard_map/ppermute | solution.py:27
  105.6 36.7 %collective-permute-start.14 = (bf16[1,512,256]{2,1,0:T(8,128)(2,1)}, bf16[1,512,256]{2,1,0:T(8,128)(2,1)}, u32[]{:S(2)}, u32[]{:S(2)}) collective-permute-start(bf16[1,512,256]{2,1,0:T(8,128)(2,1)} %copy-done.6), channel_id=1, source_target_pairs={{0,6},{1,7},{2,4},{3,5},{4,2},{5,3},{6,0},{7,1},{8,14},{9,15},{10,... | collective-permute-start | bytes 786440 | tf_op jit(solution)/shard_map/ppermute | solution.py:27
  108.1 16.0 %collective-permute-start.17 = (bf16[1,512,256]{2,1,0:T(8,128)(2,1)}, bf16[1,512,256]{2,1,0:T(8,128)(2,1)S(1)}, u32[]{:S(2)}, u32[]{:S(2)}) collective-permute-start(bf16[1,512,256]{2,1,0:T(8,128)(2,1)} %copy-done.8), channel_id=1, source_target_pairs={{0,2},{1,3},{2,0},{3,1},{4,6},{5,7},{6,4},{7,5},{8,10},{9,11},{10,... | collective-permute-start | bytes 786440 | tf_op jit(solution)/shard_map/ppermute | solution.py:27
  121.4 16.6 %collective-permute-start.16 = (bf16[1,512,256]{2,1,0:T(8,128)(2,1)S(1)}, bf16[1,512,256]{2,1,0:T(8,128)(2,1)S(1)}, u32[]{:S(2)}, u32[]{:S(2)}) collective-permute-start(bf16[1,512,256]{2,1,0:T(8,128)(2,1)S(1)} %get-tuple-element.28), channel_id=1, source_target_pairs={{0,6},{1,7},{2,4},{3,5},{4,2},{5,3},{6,0},{7,1},{8,14},{9,15},{10,... | collective-permute-start | bytes 786440 | tf_op jit(solution)/shard_map/ppermute | solution.py:27
  123.1 14.7 %collective-permute-start.20 = (bf16[16,16,130]{2,1,0:T(8,128)(2,1)S(1)}, bf16[16,16,130]{2,1,0:T(8,128)(2,1)S(1)}, u32[]{:S(2)}, u32[]{:S(2)}) collective-permute-start(bf16[16,16,130]{2,1,0:T(8,128)(2,1)S(1)} %get-tuple-element.43.refs_8_), channel_id=1, source_target_pairs={{0,2},{1,3},{2,0},{3,1},{4,6},{5,7},{6,4},{7,5},{8,10},{9,11},{10,... | collective-permute-start | bytes 199688 | tf_op jit(solution)/shard_map/ppermute | solution.py:27
  124.1 13.9 %collective-permute-start.18 = (bf16[1,512,256]{2,1,0:T(8,128)(2,1)S(1)}, bf16[1,512,256]{2,1,0:T(8,128)(2,1)S(1)}, u32[]{:S(2)}, u32[]{:S(2)}) collective-permute-start(bf16[1,512,256]{2,1,0:T(8,128)(2,1)S(1)} %collective-permute-done.17), channel_id=1, source_target_pairs={{0,6},{1,7},{2,4},{3,5},{4,2},{5,3},{6,0},{7,1},{8,14},{9,15},{10,... | collective-permute-start | bytes 786440 | tf_op jit(solution)/shard_map/ppermute | solution.py:27
  138.0 4.8 %copy-start.12 = (f32[16,1,1024]{2,1,0:T(1,128)S(1)}, f32[16,1,1024]{2,1,0:T(1,128)}, u32[]{:S(2)}) copy-start(f32[16,1,1024]{2,1,0:T(1,128)} %get-tuple-element.62) | copy-start | bytes 196612
  139.1 11.7 %collective-permute-start.19 = (bf16[4,512,256]{2,1,0:T(8,128)(2,1)}, bf16[4,512,256]{2,1,0:T(8,128)(2,1)S(1)}, u32[]{:S(2)}, u32[]{:S(2)}) collective-permute-start(bf16[4,512,256]{2,1,0:T(8,128)(2,1)} %pad_maximum_fusion), channel_id=1, source_target_pairs={{0,1},{1,0},{2,3},{3,2},{4,5},{5,4},{6,7},{7,6},{8,9},{9,8},{10,11... | collective-permute-start | bytes 3145736 | tf_op jit(solution)/shard_map/ppermute | solution.py:27
  139.5 2.7 %collective-permute-start.21 = (bf16[16,16,130]{2,1,0:T(8,128)(2,1)S(1)}, bf16[16,16,130]{2,1,0:T(8,128)(2,1)S(1)}, u32[]{:S(2)}, u32[]{:S(2)}) collective-permute-start(bf16[16,16,130]{2,1,0:T(8,128)(2,1)S(1)} %get-tuple-element.40), channel_id=1, source_target_pairs={{0,1},{1,0},{2,3},{3,2},{4,5},{5,4},{6,7},{7,6},{8,9},{9,8},{10,11... | collective-permute-start | bytes 199688 | tf_op jit(solution)/shard_map/ppermute | solution.py:27
  140.3 9.7 %collective-permute-start.13 = (bf16[1,512,256]{2,1,0:T(8,128)(2,1)}, bf16[1,512,256]{2,1,0:T(8,128)(2,1)S(1)}, u32[]{:S(2)}, u32[]{:S(2)}) collective-permute-start(bf16[1,512,256]{2,1,0:T(8,128)(2,1)} %copy-done.7), channel_id=1, source_target_pairs={{0,6},{1,7},{2,4},{3,5},{4,2},{5,3},{6,0},{7,1},{8,14},{9,15},{10,... | collective-permute-start | bytes 786440 | tf_op jit(solution)/shard_map/ppermute | solution.py:27
  142.2 8.6 %collective-permute-start.15 = (bf16[1,512,256]{2,1,0:T(8,128)(2,1)}, bf16[1,512,256]{2,1,0:T(8,128)(2,1)S(1)}, u32[]{:S(2)}, u32[]{:S(2)}) collective-permute-start(bf16[1,512,256]{2,1,0:T(8,128)(2,1)} %collective-permute-done.14), channel_id=1, source_target_pairs={{0,2},{1,3},{2,0},{3,1},{4,6},{5,7},{6,4},{7,5},{8,10},{9,11},{10,... | collective-permute-start | bytes 786440 | tf_op jit(solution)/shard_map/ppermute | solution.py:27
  (9 other events, 15.2 us)

commit v2 on v1

--- a/solution.py
+++ b/solution.py
@@ -531,6 +531,7 @@
     back_5, back_4 = swap(out_5, 2), swap(out_4, 6)
     back_32 = swap(out_32, 2)
     back = decode_order(source_rep, after(back, token))
+    back = packed(*merge(back, swap(back, 1)))
     other = swap(back, 6)
     out_0, out_7, token = part(
         table,
@@ -549,11 +550,9 @@
         table, keyed, [query_a2, query_x, back, token], [(7, 0, None), (6, 0, None)], [1, 6], [1, 1]
     )
     back_6 = swap(out_6, 6)
-    back = packed(*merge(back, after(other, token)))
-    other = swap(back, 1)
     back_x = swap(jnp.concatenate([out_1, back_32[0:1], back_7, back_5]), 1)
     pre_out = prefill_join(table, [out_0, back_32, back_6, back_4, back_x])
-    weighted, top, total = merge(back, other)
+    weighted, top, total = merge(back, after(other, token))
     dec_out = decode_finish(weighted, top, total, dec_query, dec_own)
     return (pre_out, dec_out)
 

time: 154 us -> 154 us (level)
  the two profiles are of different devices: /device:TPU:2 before, /device:TPU:0 now
where the time goes in v2:
time: 154 us
  Pallas kernels  44.9 us (29%)
  starting transfers between devices  40.5 us (26%)
  waiting for transfers between devices  36.3 us (24%)
  local copies, waits for them, and re-layouts  15.8 us (10%)
  other arithmetic  13.7 us (9%)
  between operations  2.07 us (1%)
    pallas_call x3, Pallas kernels, attend_call(): pl.pallas_call(kernel, grid_spec=pltpu.PrefetchScalarGridSpec(num_scalar_...  34.1 us
    ppermute x22, starting transfers between devices, swap(): return lax.ppermute(array, 'ctx', [(i, i ^ flip) for i in range(8)])  28.2 us
    ppermute x22, waiting for transfers between devices, swap(): return lax.ppermute(array, 'ctx', [(i, i ^ flip) for i in range(8)])  23.2 us
    all_to_all x2, waiting for transfers between devices, exchange(): return lax.all_to_all(array, 'rep', split_axis=0, concat_axis=0, tiled=True)  13.1 us
    all_to_all x2, starting transfers between devices, exchange(): return lax.all_to_all(array, 'rep', split_axis=0, concat_axis=0, tiled=True)  12.3 us
    unnamed x42, local copies, waits for them, and re-layouts  6.29 us
    pallas_call x1, Pallas kernels, over_cache(): pl.pallas_call(cache_kernel, grid_spec=pltpu.PrefetchScalarGridSpec(num_s...  5.82 us
    pallas_call x2, Pallas kernels, collect(): pl.pallas_call(functools.partial(collect_kernel, outs=outs, count_in=len(...  4.99 us
  transfers between devices with their start and end apart: 24, of which 8 were waited for; matrix products, arithmetic and copies ran while one was open for 15% of the time, Pallas kernels for 15%

profile of v2, /device:TPU:0, one launch (start us, length us, event | category | flops | bytes accessed | tf_op | source)
XLA Modules:
  0.0 153.6 jit_solution(9164222326859538537)
XLA Ops:
  0.7 2.3 %dynamic-slice_bitcast_fusion = (bf16[1,512,256]{2,1,0:T(8,128)(2,1)S(1)}, bf16[1,512,256]{2,1,0:T(8,128)(2,1)S(1)}, bf16[1,512,256]{2,1,0:T(8,128)(2,1)}, bf16[...) fusion(bf16[1,2,512,1024]{3,2,1,0:T(8,128)(2,1)} %param.9, ...), kind=kLoop, calls=%fused_computation.12 | loop fusion | bytes 3145740 | tf_op jit(solution)/shard_map/squeeze | solution.py:274
  3.8 1.7 %collective-permute-start = (bf16[2,512,256]{2,1,0:T(8,128)(2,1)}, bf16[2,512,256]{2,1,0:T(8,128)(2,1)S(1)}, u32[]{:S(2)}, u32[]{:S(2)}) collective-permute-start(bf16[2,512,256]{2,1,0:T(8,128)(2,1)} %pad_maximum_fusion.1), channel_id=1, source_target_pairs={{0,2},{1,3},{2,0},{3,1},{4,6},{5,7},{6,4},{7,5},{8,10},{9,11},{10,... | collective-permute-start | bytes 1572872 | tf_op jit(solution)/shard_map/ppermute | solution.py:27
  6.4 2.2 %collective-permute-start.2 = (bf16[2,512,256]{2,1,0:T(8,128)(2,1)}, bf16[2,512,256]{2,1,0:T(8,128)(2,1)S(1)}, u32[]{:S(2)}, u32[]{:S(2)}) collective-permute-start(bf16[2,512,256]{2,1,0:T(8,128)(2,1)} %pad_maximum_fusion.3), channel_id=1, source_target_pairs={{0,6},{1,7},{2,4},{3,5},{4,2},{5,3},{6,0},{7,1},{8,14},{9,15},{10,... | collective-permute-start | bytes 1572872 | tf_op jit(solution)/shard_map/ppermute | solution.py:27
  11.5 7.3 %collective-permute-done.refs_1_ = bf16[2,512,256]{2,1,0:T(8,128)(2,1)S(1)} collective-permute-done((bf16[2,512,256]{2,1,0:T(8,128)(2,1)}, bf16[2,512,256]{2,1,0:T(8,128)(2,1)S(1)}, u32[]{:S(2)}, u32[]{:S(2)}) %collective-permute-start) | collective-permute-done | bytes 524320 | tf_op jit(solution)/shard_map/ppermute | solution.py:27
  19.7 3.1 %collective-permute-start.1 = (bf16[2,512,256]{2,1,0:T(8,128)(2,1)}, bf16[2,512,256]{2,1,0:T(8,128)(2,1)}, u32[]{:S(2)}, u32[]{:S(2)}) collective-permute-start(bf16[2,512,256]{2,1,0:T(8,128)(2,1)} %pad_maximum_fusion.2), channel_id=1, source_target_pairs={{0,6},{1,7},{2,4},{3,5},{4,2},{5,3},{6,0},{7,1},{8,14},{9,15},{10,... | collective-permute-start | bytes 1572872 | tf_op jit(solution)/shard_map/ppermute | solution.py:27
  23.9 1.2 constant_dynamic-slice_fusion.2
  25.1 1.0 collective-permute-start.6
  28.9 7.9 %all-to-all-start = ((bf16[16,2,1024]{2,1,0:T(2,128)(2,1)}), bf16[16,2,1024]{2,1,0:T(2,128)(2,1)}, u32[]{:S(2)}, u32[]{:S(2)}) async-start(bf16[16,2,1024]{2,1,0:T(2,128)(2,1)} %reshape.110), calls=%async_computation | async-start | bytes 131072 | tf_op jit(solution)/shard_map/all_to_all | solution.py:31
  38.7 5.8 %all-to-all-done = bf16[16,2,1024]{2,1,0:T(2,128)(2,1)} async-done(((bf16[16,2,1024]{2,1,0:T(2,128)(2,1)}), bf16[16,2,1024]{2,1,0:T(2,128)(2,1)}, u32[]{:S(2)}, u32[]{:S(2)}) %all-to-all-start) | async-done | bytes 65568 | tf_op jit(solution)/shard_map/all_to_all | solution.py:31
  45.5 1.0 slice.111
  46.5 2.8 %shard_map.95 = bf16[8,512,128]{2,1,0:T(8,128)(2,1)} custom-call(s32[2]{0:T(128)S(1)} %pad_add_fusion.table, bf16[2,512,1024]{2,1,0:T(8,128)(2,1)S(1)} %bitcast.36, bf16[2,512,256]{2,1,0:T(8,128)(2,1)S(1)} %collective-permute-done.refs_1_, bf16[2,512,256]{2,1,0:T(8,128)(2,1)} %collective-permute-done.1.refs_2_, ...), custom_call_target="tpu_custom_call" | custom-call | flops 1048576 | bytes 2097152 | tf_op jit(solution)/shard_map/pallas_call | solution.py:247
  50.2 2.3 %collective-permute-start.8 = (bf16[2,512,256]{2,1,0:T(8,128)(2,1)}, bf16[2,512,256]{2,1,0:T(8,128)(2,1)}, u32[]{:S(2)}, u32[]{:S(2)}) collective-permute-start(bf16[2,512,256]{2,1,0:T(8,128)(2,1)} %pad_maximum_fusion.8), channel_id=1, source_target_pairs={{0,6},{1,7},{2,4},{3,5},{4,2},{5,3},{6,0},{7,1},{8,14},{9,15},{10,... | collective-permute-start | bytes 1572872 | tf_op jit(solution)/shard_map/ppermute | solution.py:27
  53.5 1.0 slice.112
  55.9 5.8 %over_cache.1 = bf16[16,16,256]{2,1,0:T(8,128)(2,1)S(1)} custom-call(s32[33]{0:T(128)S(1)} %pad_add_fusion.1.table, bf16[16,16,128]{2,1,0:T(8,128)(2,1)S(1)} %bitcast.43, bf16[16,2,128,1024]{3,2,1,0:T(8,128)(2,1)} %cache_ref.1), custom_call_target="tpu_custom_call" | custom-call | flops 8000000000 | bytes 8500000 | tf_op jit(solution)/shard_map/over_cache/pallas_call | solution.py:406
  62.0 1.0 reduce.19
  63.8 4.3 %all-to-all-start.1 = ((bf16[16,2,1040]{2,1,0:T(2,128)(2,1)}), bf16[16,2,1040]{2,1,0:T(2,128)(2,1)}, u32[]{:S(2)}, u32[]{:S(2)}) async-start(bf16[16,2,1040]{2,1,0:T(2,128)(2,1)} %reshape.112), calls=%async_computation.1 | async-start | bytes 147456 | tf_op jit(solution)/shard_map/all_to_all | solution.py:31
  68.3 7.3 %all-to-all-done.1 = bf16[16,2,1040]{2,1,0:T(2,128)(2,1)} async-done(((bf16[16,2,1040]{2,1,0:T(2,128)(2,1)}), bf16[16,2,1040]{2,1,0:T(2,128)(2,1)}, u32[]{:S(2)}, u32[]{:S(2)}) %all-to-all-start.1) | async-done | bytes 66592 | tf_op jit(solution)/shard_map/all_to_all | solution.py:31
  75.6 1.0 reshape.113
  76.7 19.0 %shard_map.96 = (bf16[1,512,256]{2,1,0:T(8,128)(2,1)S(1)}, bf16[1,512,256]{2,1,0:T(8,128)(2,1)S(1)}, bf16[2,512,256]{2,1,0:T(8,128)(2,1)S(1)}, f32[8,128]{1,0:T(8,128)S(1)}) custom-call(s32[2]{0:T(128)S(1)} %pad_add_fusion.table, bf16[2,512,1024]{2,1,0:T(8,128)(2,1)S(1)} %bitcast.37, bf16[2,512,256]{2,1,0:T(8,128)(2,1)S(1)} %collective-permute-done.refs_1_, ...), custom_call_target="tpu_custom_call" | custom-call | flops 4800000000 | bytes 4000000 | tf_op jit(solution)/shard_map/pallas_call | solution.py:186
  98.7 2.0 %collective-permute-start.18 = (bf16[1,512,256]{2,1,0:T(8,128)(2,1)}, bf16[1,512,256]{2,1,0:T(8,128)(2,1)S(1)}, u32[]{:S(2)}, u32[]{:S(2)}) collective-permute-start(bf16[1,512,256]{2,1,0:T(8,128)(2,1)} %copy-done.9), channel_id=1, source_target_pairs={{0,2},{1,3},{2,0},{3,1},{4,6},{5,7},{6,4},{7,5},{8,10},{9,11},{10,... | collective-permute-start | bytes 786440 | tf_op jit(solution)/shard_map/ppermute | solution.py:27
  102.3 3.9 %shard_map.97 = (bf16[1,512,256]{2,1,0:T(8,128)(2,1)S(1)}, bf16[1,512,256]{2,1,0:T(8,128)(2,1)S(1)}, f32[8,128]{1,0:T(8,128)S(1)}) custom-call(s32[2]{0:T(128)S(1)} %pad_add_fusion.table, bf16[2,512,1024]{2,1,0:T(8,128)(2,1)S(1)} %bitcast.38, bf16[2,512,256]{2,1,0:T(8,128)(2,1)S(1)} %collective-permute-done.refs_1_, ...), custom_call_target="tpu_custom_call" | custom-call | flops 2400000000 | bytes 4000000 | tf_op jit(solution)/shard_map/pallas_call | solution.py:186
  106.2 9.3 %collective-permute-start.17 = (bf16[1,512,256]{2,1,0:T(8,128)(2,1)S(1)}, bf16[1,512,256]{2,1,0:T(8,128)(2,1)S(1)}, u32[]{:S(2)}, u32[]{:S(2)}) collective-permute-start(bf16[1,512,256]{2,1,0:T(8,128)(2,1)S(1)} %get-tuple-element.28), channel_id=1, source_target_pairs={{0,6},{1,7},{2,4},{3,5},{4,2},{5,3},{6,0},{7,1},{8,14},{9,15},{10,... | collective-permute-start | bytes 786440 | tf_op jit(solution)/shard_map/ppermute | solution.py:27
  115.9 3.0 %collective-permute-done.18 = bf16[1,512,256]{2,1,0:T(8,128)(2,1)S(1)} collective-permute-done((bf16[1,512,256]{2,1,0:T(8,128)(2,1)}, bf16[1,512,256]{2,1,0:T(8,128)(2,1)S(1)}, u32[]{:S(2)}, u32[]{:S(2)}) %collective-permute-start.18) | collective-permute-done | bytes 262176 | tf_op jit(solution)/shard_map/ppermute | solution.py:27
  120.3 11.1 %shard_map.98 = (bf16[1,512,256]{2,1,0:T(8,128)(2,1)S(1)}, bf16[1,512,256]{2,1,0:T(8,128)(2,1)S(1)}, f32[8,128]{1,0:T(8,128)}) custom-call(s32[2]{0:T(128)S(1)} %pad_add_fusion.table, bf16[2,512,1024]{2,1,0:T(8,128)(2,1)S(1)} %bitcast.39, bf16[2,512,256]{2,1,0:T(8,128)(2,1)S(1)} %collective-permute-done.refs_1_, ...), custom_call_target="tpu_custom_call" | custom-call | flops 2400000000 | bytes 4000000 | tf_op jit(solution)/shard_map/pallas_call | solution.py:186
  131.6 1.1 pad_maximum_fusion
  132.9 2.0 %collective-permute-start.15 = (bf16[1,512,256]{2,1,0:T(8,128)(2,1)S(1)}, bf16[1,512,256]{2,1,0:T(8,128)(2,1)}, u32[]{:S(2)}, u32[]{:S(2)}) collective-permute-start(bf16[1,512,256]{2,1,0:T(8,128)(2,1)S(1)} %copy-done.7), channel_id=1, source_target_pairs={{0,6},{1,7},{2,4},{3,5},{4,2},{5,3},{6,0},{7,1},{8,14},{9,15},{10,... | collective-permute-start | bytes 786440 | tf_op jit(solution)/shard_map/ppermute | solution.py:27
  135.6 1.4 collective-permute-start.14
  136.9 3.6 %collective-permute-done.21 = bf16[16,16,130]{2,1,0:T(8,128)(2,1)S(1)} collective-permute-done((bf16[16,16,130]{2,1,0:T(8,128)(2,1)S(1)}, bf16[16,16,130]{2,1,0:T(8,128)(2,1)S(1)}, u32[]{:S(2)}, u32[]{:S(2)}) %collective-permute-start.21) | collective-permute-done | bytes 66592 | tf_op jit(solution)/shard_map/ppermute | solution.py:27
  140.5 3.0 %collective-permute-done.15 = bf16[1,512,256]{2,1,0:T(8,128)(2,1)} collective-permute-done((bf16[1,512,256]{2,1,0:T(8,128)(2,1)S(1)}, bf16[1,512,256]{2,1,0:T(8,128)(2,1)}, u32[]{:S(2)}, u32[]{:S(2)}) %collective-permute-start.15) | collective-permute-done | bytes 262176 | tf_op jit(solution)/shard_map/ppermute | solution.py:27
  144.8 3.7 %collective-permute-done.14.refs_2_ = bf16[1,512,256]{2,1,0:T(8,128)(2,1)S(1)} collective-permute-done((bf16[1,512,256]{2,1,0:T(8,128)(2,1)}, bf16[1,512,256]{2,1,0:T(8,128)(2,1)S(1)}, u32[]{:S(2)}, u32[]{:S(2)}) %collective-permute-start.14) | collective-permute-done | bytes 262176 | tf_op jit(solution)/shard_map/ppermute | solution.py:27
  148.6 2.6 %collective-permute-done.16.refs_3_ = bf16[1,512,256]{2,1,0:T(8,128)(2,1)S(1)} collective-permute-done((bf16[1,512,256]{2,1,0:T(8,128)(2,1)}, bf16[1,512,256]{2,1,0:T(8,128)(2,1)S(1)}, u32[]{:S(2)}, u32[]{:S(2)}) %collective-permute-start.16) | collective-permute-done | bytes 262176 | tf_op jit(solution)/shard_map/ppermute | solution.py:27
  151.1 2.2 %shard_map.99 = bf16[1,512,2048]{2,1,0:T(8,128)(2,1)} custom-call(s32[2]{0:T(128)S(1)} %pad_add_fusion.table, bf16[1,512,256]{2,1,0:T(8,128)(2,1)S(1)} %get-tuple-element.22.refs_0_, bf16[2,512,256]{2,1,0:T(8,128)(2,1)S(1)} %collective-permute-done.12.refs_1_, bf16[1,512,256]{2,1,0:T(8,128)(2,1)S(1)} %collective-permute-done.14.refs_2_, ...), custom_call_target="tpu_custom_call" | custom-call | flops 2097152 | bytes 4194304 | tf_op jit(solution)/shard_map/pallas_call | solution.py:247
  (120 shorter events, 24.5 us)
Async XLA Ops:
  0.7 7.9 %copy-start.1 = (bf16[1,512,2048]{2,1,0:T(8,128)(2,1)S(1)}, bf16[1,512,2048]{2,1,0:T(8,128)(2,1)}, u32[]{:S(2)}) copy-start(bf16[1,512,2048]{2,1,0:T(8,128)(2,1)} %param.8) | copy-start | bytes 6291460
  3.8 15.0 %collective-permute-start = (bf16[2,512,256]{2,1,0:T(8,128)(2,1)}, bf16[2,512,256]{2,1,0:T(8,128)(2,1)S(1)}, u32[]{:S(2)}, u32[]{:S(2)}) collective-permute-start(bf16[2,512,256]{2,1,0:T(8,128)(2,1)} %pad_maximum_fusion.1), channel_id=1, source_target_pairs={{0,2},{1,3},{2,0},{3,1},{4,6},{5,7},{6,4},{7,5},{8,10},{9,11},{10,... | collective-permute-start | bytes 1572872 | tf_op jit(solution)/shard_map/ppermute | solution.py:27
  6.4 16.5 %collective-permute-start.2 = (bf16[2,512,256]{2,1,0:T(8,128)(2,1)}, bf16[2,512,256]{2,1,0:T(8,128)(2,1)S(1)}, u32[]{:S(2)}, u32[]{:S(2)}) collective-permute-start(bf16[2,512,256]{2,1,0:T(8,128)(2,1)} %pad_maximum_fusion.3), channel_id=1, source_target_pairs={{0,6},{1,7},{2,4},{3,5},{4,2},{5,3},{6,0},{7,1},{8,14},{9,15},{10,... | collective-permute-start | bytes 1572872 | tf_op jit(solution)/shard_map/ppermute | solution.py:27
  8.7 10.2 %copy-start.11 = (bf16[1,512,256]{2,1,0:T(8,128)(2,1)S(1)}, bf16[1,512,256]{2,1,0:T(8,128)(2,1)}, u32[]{:S(2)}) copy-start(bf16[1,512,256]{2,1,0:T(8,128)(2,1)} %get-tuple-element.53) | copy-start | bytes 786436
  9.5 15.6 %collective-permute-start.5 = (bf16[2,512,256]{2,1,0:T(8,128)(2,1)}, bf16[2,512,256]{2,1,0:T(8,128)(2,1)}, u32[]{:S(2)}, u32[]{:S(2)}) collective-permute-start(bf16[2,512,256]{2,1,0:T(8,128)(2,1)} %pad_maximum_fusion.5), channel_id=1, source_target_pairs={{0,1},{1,0},{2,3},{3,2},{4,5},{5,4},{6,7},{7,6},{8,9},{9,8},{10,11... | collective-permute-start | bytes 1572872 | tf_op jit(solution)/shard_map/ppermute | solution.py:27
  10.4 35.1 %collective-permute-start.7 = (bf16[2,512,256]{2,1,0:T(8,128)(2,1)}, bf16[2,512,256]{2,1,0:T(8,128)(2,1)}, u32[]{:S(2)}, u32[]{:S(2)}) collective-permute-start(bf16[2,512,256]{2,1,0:T(8,128)(2,1)} %pad_maximum_fusion.6), channel_id=1, source_target_pairs={{0,2},{1,3},{2,0},{3,1},{4,6},{5,7},{6,4},{7,5},{8,10},{9,11},{10,... | collective-permute-start | bytes 1572872 | tf_op jit(solution)/shard_map/ppermute | solution.py:27
  19.7 17.8 %copy-start.16 = (s32[256]{0:T(256)S(1)}, s32[256]{0:T(256)}, u32[]{:S(2)}) copy-start(s32[256]{0:T(256)} %param.14) | copy-start | bytes 3076
  19.7 26.8 %collective-permute-start.1 = (bf16[2,512,256]{2,1,0:T(8,128)(2,1)}, bf16[2,512,256]{2,1,0:T(8,128)(2,1)}, u32[]{:S(2)}, u32[]{:S(2)}) collective-permute-start(bf16[2,512,256]{2,1,0:T(8,128)(2,1)} %pad_maximum_fusion.2), channel_id=1, source_target_pairs={{0,6},{1,7},{2,4},{3,5},{4,2},{5,3},{6,0},{7,1},{8,14},{9,15},{10,... | collective-permute-start | bytes 1572872 | tf_op jit(solution)/shard_map/ppermute | solution.py:27
  22.8 53.8 %copy-start.3 = (bf16[2,512,256]{2,1,0:T(8,128)(2,1)}, bf16[2,512,256]{2,1,0:T(8,128)(2,1)S(1)}, u32[]{:S(2)}) copy-start(bf16[2,512,256]{2,1,0:T(8,128)(2,1)S(1)} %collective-permute-done.2.refs_3_) | copy-start | bytes 1572868
  23.8 22.7 %copy-start = (bf16[1,2,512,1024]{3,2,1,0:T(8,128)(2,1)S(1)}, bf16[1,2,512,1024]{3,2,1,0:T(8,128)(2,1)}, u32[]{:S(2)}) copy-start(bf16[1,2,512,1024]{3,2,1,0:T(8,128)(2,1)} %param.9) | copy-start | bytes 6291460
  23.8 22.7 %collective-permute-start.3 = (bf16[2,512,256]{2,1,0:T(8,128)(2,1)}, bf16[2,512,256]{2,1,0:T(8,128)(2,1)}, u32[]{:S(2)}, u32[]{:S(2)}) collective-permute-start(bf16[2,512,256]{2,1,0:T(8,128)(2,1)} %pad_maximum_fusion.4), channel_id=1, source_target_pairs={{0,2},{1,3},{2,0},{3,1},{4,6},{5,7},{6,4},{7,5},{8,10},{9,11},{10,... | collective-permute-start | bytes 1572872 | tf_op jit(solution)/shard_map/ppermute | solution.py:27
  25.1 27.4 %collective-permute-start.6 = (bf16[2,512,256]{2,1,0:T(8,128)(2,1)}, bf16[2,512,256]{2,1,0:T(8,128)(2,1)}, u32[]{:S(2)}, u32[]{:S(2)}) collective-permute-start(bf16[2,512,256]{2,1,0:T(8,128)(2,1)} %collective-permute-done.5), channel_id=1, source_target_pairs={{0,6},{1,7},{2,4},{3,5},{4,2},{5,3},{6,0},{7,1},{8,14},{9,15},{10,... | collective-permute-start | bytes 1572872 | tf_op jit(solution)/shard_map/ppermute | solution.py:27
  27.0 26.5 %collective-permute-start.9 = (bf16[2,512,256]{2,1,0:T(8,128)(2,1)}, bf16[2,512,256]{2,1,0:T(8,128)(2,1)}, u32[]{:S(2)}, u32[]{:S(2)}) collective-permute-start(bf16[2,512,256]{2,1,0:T(8,128)(2,1)} %pad_maximum_fusion.7), channel_id=1, source_target_pairs={{0,1},{1,0},{2,3},{3,2},{4,5},{5,4},{6,7},{7,6},{8,9},{9,8},{10,11... | collective-permute-start | bytes 1572872 | tf_op jit(solution)/shard_map/ppermute | solution.py:27
  28.9 15.7 %all-to-all-start = ((bf16[16,2,1024]{2,1,0:T(2,128)(2,1)}), bf16[16,2,1024]{2,1,0:T(2,128)(2,1)}, u32[]{:S(2)}, u32[]{:S(2)}) async-start(bf16[16,2,1024]{2,1,0:T(2,128)(2,1)} %reshape.110), calls=%async_computation | async-start | bytes 131072 | tf_op jit(solution)/shard_map/all_to_all | solution.py:31
  49.3 27.4 %collective-permute-start.4 = (bf16[8,512,128]{2,1,0:T(8,128)(2,1)}, bf16[8,512,128]{2,1,0:T(8,128)(2,1)}, u32[]{:S(2)}, u32[]{:S(2)}) collective-permute-start(bf16[8,512,128]{2,1,0:T(8,128)(2,1)} %shard_map.95), channel_id=1, source_target_pairs={{0,1},{1,0},{2,3},{3,2},{4,5},{5,4},{6,7},{7,6},{8,9},{9,8},{10,11... | collective-permute-start | bytes 3145736 | tf_op jit(solution)/shard_map/ppermute | solution.py:27
  50.2 26.4 %collective-permute-start.8 = (bf16[2,512,256]{2,1,0:T(8,128)(2,1)}, bf16[2,512,256]{2,1,0:T(8,128)(2,1)}, u32[]{:S(2)}, u32[]{:S(2)}) collective-permute-start(bf16[2,512,256]{2,1,0:T(8,128)(2,1)} %pad_maximum_fusion.8), channel_id=1, source_target_pairs={{0,6},{1,7},{2,4},{3,5},{4,2},{5,3},{6,0},{7,1},{8,14},{9,15},{10,... | collective-permute-start | bytes 1572872 | tf_op jit(solution)/shard_map/ppermute | solution.py:27
  55.4 21.3 %collective-permute-start.10 = (bf16[2,512,256]{2,1,0:T(8,128)(2,1)}, bf16[2,512,256]{2,1,0:T(8,128)(2,1)}, u32[]{:S(2)}, u32[]{:S(2)}) collective-permute-start(bf16[2,512,256]{2,1,0:T(8,128)(2,1)} %pad_maximum_fusion.9), channel_id=1, source_target_pairs={{0,2},{1,3},{2,0},{3,1},{4,6},{5,7},{6,4},{7,5},{8,10},{9,11},{10,... | collective-permute-start | bytes 1572872 | tf_op jit(solution)/shard_map/ppermute | solution.py:27
  63.8 11.8 %all-to-all-start.1 = ((bf16[16,2,1040]{2,1,0:T(2,128)(2,1)}), bf16[16,2,1040]{2,1,0:T(2,128)(2,1)}, u32[]{:S(2)}, u32[]{:S(2)}) async-start(bf16[16,2,1040]{2,1,0:T(2,128)(2,1)} %reshape.112), calls=%async_computation.1 | async-start | bytes 147456 | tf_op jit(solution)/shard_map/all_to_all | solution.py:31
  98.5 3.8 %copy-start.2 = (bf16[1,512,2048]{2,1,0:T(8,128)(2,1)S(1)}, bf16[1,512,2048]{2,1,0:T(8,128)(2,1)}, u32[]{:S(2)}) copy-start(bf16[1,512,2048]{2,1,0:T(8,128)(2,1)} %param.8) | copy-start | bytes 6291460
  98.5 3.7 %copy-start.4 = (bf16[2,512,256]{2,1,0:T(8,128)(2,1)S(1)}, bf16[2,512,256]{2,1,0:T(8,128)(2,1)}, u32[]{:S(2)}) copy-start(bf16[2,512,256]{2,1,0:T(8,128)(2,1)} %copy-done.3) | copy-start | bytes 1572868
  98.5 2.2 %collective-permute-start.11 = (bf16[16,16,130]{2,1,0:T(8,128)(2,1)S(1)}, bf16[16,16,130]{2,1,0:T(8,128)(2,1)S(1)}, u32[]{:S(2)}, u32[]{:S(2)}) collective-permute-start(bf16[16,16,130]{2,1,0:T(8,128)(2,1)S(1)} %reshape.96), channel_id=1, source_target_pairs={{0,1},{1,0},{2,3},{3,2},{4,5},{5,4},{6,7},{7,6},{8,9},{9,8},{10,11... | collective-permute-start | bytes 199688 | tf_op jit(solution)/shard_map/ppermute | solution.py:27
  98.7 32.8 %collective-permute-start.12 = (bf16[2,512,256]{2,1,0:T(8,128)(2,1)}, bf16[2,512,256]{2,1,0:T(8,128)(2,1)S(1)}, u32[]{:S(2)}, u32[]{:S(2)}) collective-permute-start(bf16[2,512,256]{2,1,0:T(8,128)(2,1)} %copy-done.5), channel_id=1, source_target_pairs={{0,2},{1,3},{2,0},{3,1},{4,6},{5,7},{6,4},{7,5},{8,10},{9,11},{10,... | collective-permute-start | bytes 1572872 | tf_op jit(solution)/shard_map/ppermute | solution.py:27
  98.7 20.1 %collective-permute-start.18 = (bf16[1,512,256]{2,1,0:T(8,128)(2,1)}, bf16[1,512,256]{2,1,0:T(8,128)(2,1)S(1)}, u32[]{:S(2)}, u32[]{:S(2)}) collective-permute-start(bf16[1,512,256]{2,1,0:T(8,128)(2,1)} %copy-done.9), channel_id=1, source_target_pairs={{0,2},{1,3},{2,0},{3,1},{4,6},{5,7},{6,4},{7,5},{8,10},{9,11},{10,... | collective-permute-start | bytes 786440 | tf_op jit(solution)/shard_map/ppermute | solution.py:27
  101.3 14.1 %collective-permute-start.13 = (bf16[16,16,130]{2,1,0:T(8,128)(2,1)S(1)}, bf16[16,16,130]{2,1,0:T(8,128)(2,1)S(1)}, u32[]{:S(2)}, u32[]{:S(2)}) collective-permute-start(bf16[16,16,130]{2,1,0:T(8,128)(2,1)S(1)} %get-tuple-element.43.refs_8_), channel_id=1, source_target_pairs={{0,6},{1,7},{2,4},{3,5},{4,2},{5,3},{6,0},{7,1},{8,14},{9,15},{10,... | collective-permute-start | bytes 199688 | tf_op jit(solution)/shard_map/ppermute | solution.py:27
  106.2 25.4 %collective-permute-start.17 = (bf16[1,512,256]{2,1,0:T(8,128)(2,1)S(1)}, bf16[1,512,256]{2,1,0:T(8,128)(2,1)S(1)}, u32[]{:S(2)}, u32[]{:S(2)}) collective-permute-start(bf16[1,512,256]{2,1,0:T(8,128)(2,1)S(1)} %get-tuple-element.28), channel_id=1, source_target_pairs={{0,6},{1,7},{2,4},{3,5},{4,2},{5,3},{6,0},{7,1},{8,14},{9,15},{10,... | collective-permute-start | bytes 786440 | tf_op jit(solution)/shard_map/ppermute | solution.py:27
  118.9 12.7 %collective-permute-start.19 = (bf16[1,512,256]{2,1,0:T(8,128)(2,1)S(1)}, bf16[1,512,256]{2,1,0:T(8,128)(2,1)S(1)}, u32[]{:S(2)}, u32[]{:S(2)}) collective-permute-start(bf16[1,512,256]{2,1,0:T(8,128)(2,1)S(1)} %collective-permute-done.18), channel_id=1, source_target_pairs={{0,6},{1,7},{2,4},{3,5},{4,2},{5,3},{6,0},{7,1},{8,14},{9,15},{10,... | collective-permute-start | bytes 786440 | tf_op jit(solution)/shard_map/ppermute | solution.py:27
  131.5 12.0 %copy-start.10 = (f32[16,16,130]{2,1,0:T(8,128)S(1)}, f32[16,16,130]{2,1,0:T(8,128)}, u32[]{:S(2)}) copy-start(f32[16,16,130]{2,1,0:T(8,128)} %get-tuple-element.39) | copy-start | bytes 399364
  132.7 18.5 %collective-permute-start.20 = (bf16[4,512,256]{2,1,0:T(8,128)(2,1)}, bf16[4,512,256]{2,1,0:T(8,128)(2,1)S(1)}, u32[]{:S(2)}, u32[]{:S(2)}) collective-permute-start(bf16[4,512,256]{2,1,0:T(8,128)(2,1)} %pad_maximum_fusion), channel_id=1, source_target_pairs={{0,1},{1,0},{2,3},{3,2},{4,5},{5,4},{6,7},{7,6},{8,9},{9,8},{10,11... | collective-permute-start | bytes 3145736 | tf_op jit(solution)/shard_map/ppermute | solution.py:27
  132.9 10.6 %collective-permute-start.15 = (bf16[1,512,256]{2,1,0:T(8,128)(2,1)S(1)}, bf16[1,512,256]{2,1,0:T(8,128)(2,1)}, u32[]{:S(2)}, u32[]{:S(2)}) collective-permute-start(bf16[1,512,256]{2,1,0:T(8,128)(2,1)S(1)} %copy-done.7), channel_id=1, source_target_pairs={{0,6},{1,7},{2,4},{3,5},{4,2},{5,3},{6,0},{7,1},{8,14},{9,15},{10,... | collective-permute-start | bytes 786440 | tf_op jit(solution)/shard_map/ppermute | solution.py:27
  135.3 5.2 %collective-permute-start.21 = (bf16[16,16,130]{2,1,0:T(8,128)(2,1)S(1)}, bf16[16,16,130]{2,1,0:T(8,128)(2,1)S(1)}, u32[]{:S(2)}, u32[]{:S(2)}) collective-permute-start(bf16[16,16,130]{2,1,0:T(8,128)(2,1)S(1)} %get-tuple-element.40.refs_8_), channel_id=1, source_target_pairs={{0,2},{1,3},{2,0},{3,1},{4,6},{5,7},{6,4},{7,5},{8,10},{9,11},{10,... | collective-permute-start | bytes 199688 | tf_op jit(solution)/shard_map/ppermute | solution.py:27
  135.6 13.0 %collective-permute-start.14 = (bf16[1,512,256]{2,1,0:T(8,128)(2,1)}, bf16[1,512,256]{2,1,0:T(8,128)(2,1)S(1)}, u32[]{:S(2)}, u32[]{:S(2)}) collective-permute-start(bf16[1,512,256]{2,1,0:T(8,128)(2,1)} %copy-done.8), channel_id=1, source_target_pairs={{0,6},{1,7},{2,4},{3,5},{4,2},{5,3},{6,0},{7,1},{8,14},{9,15},{10,... | collective-permute-start | bytes 786440 | tf_op jit(solution)/shard_map/ppermute | solution.py:27
  143.5 7.6 %collective-permute-start.16 = (bf16[1,512,256]{2,1,0:T(8,128)(2,1)}, bf16[1,512,256]{2,1,0:T(8,128)(2,1)S(1)}, u32[]{:S(2)}, u32[]{:S(2)}) collective-permute-start(bf16[1,512,256]{2,1,0:T(8,128)(2,1)} %collective-permute-done.15), channel_id=1, source_target_pairs={{0,2},{1,3},{2,0},{3,1},{4,6},{5,7},{6,4},{7,5},{8,10},{9,11},{10,... | collective-permute-start | bytes 786440 | tf_op jit(solution)/shard_map/ppermute | solution.py:27
  (9 other events, 12.8 us)
